TPU v7x, 256 devices: a whole 4x4x8 slice. The times are simulated.
256 devices in a mesh: grid: 128 (over x, y_hi, z, core), band: 2 (over y_lo).
Axes of the slice: x: 4, y: 4 (y_hi: 2, y_lo: 2; y = y_hi * 2 + y_lo), z: 8, core: 2. Of those that a mesh axis runs over, the one named last changes fastest.
Arguments:
- left_bands: float32 [2, 8, 128, 128, 128], P(None, 'band', 'grid'), may hold values from -6 to 6
- right_bands: float32 [2, 4, 128, 128, 128], P(None, 'band', 'grid'), may hold values from -6 to 6
- sphere_index: int32 [16384], replicated, may hold values from 0 to 2097151, as said below
- right_order: int32 [4], replicated, may hold values from 0 to 3, each once
Outputs:
- pair_density: float32 [2, 8, 4, 16384], P(None, 'band', None, 'grid')
Inputs may be any that keep to these rules, and one draw needn't show every extreme that they name: `sphere_index`: flat index (kz * 128 + ky) * 128 + kx; an index may repeat. In each aligned block of 128 entries, at most 1 entries share one value of ky, and some value is shared by exactly 1. `right_order`: each second band once.
All inputs are finite; a program needn't handle non-finite values.
Results may differ from a plain program's by a relative error of at most 0.00008.
Values sent between devices are 32-bit elements; how exact they have to be, the bound alone decides.
A program may use at most 128 MiB of HBM per device.

v0:
```python
from functools import partial
import math

import jax
import jax.numpy as jnp
from jax import lax
from jax.sharding import PartitionSpec as P

NG = 128
NX = 128
NGV = 16384


def swapped(block, axis, apart):
    count = lax.axis_size(axis)
    route = []
    for low in range(count):
        high = low | 1 << apart
        if high != low and high < count:
            route += [(low, high), (high, low)]
    return lax.ppermute(block, axis, route)


def dft_tables(length):
    counter = jnp.arange(length, dtype=jnp.int32)
    angles = (counter[:, None] * counter[None, :] % length).astype(jnp.float32) * (
        2.0 * math.pi / length
    )
    return (jnp.cos(angles), jnp.sin(angles))


def transform_axis(real_part, imag_part, cosine, sine, form):
    product = partial(jnp.einsum, form, precision=lax.Precision.HIGHEST)
    return (
        product(real_part, cosine) + product(imag_part, sine),
        product(imag_part, cosine) - product(real_part, sine),
    )


def pair_fields(left_fields, right_fields):
    real_part = (
        left_fields[0][:, None] * right_fields[0][None]
        + left_fields[1][:, None] * right_fields[1][None]
    )
    imag_part = (
        left_fields[0][:, None] * right_fields[1][None]
        - left_fields[1][:, None] * right_fields[0][None]
    )
    new_shape = (-1,) + real_part.shape[2:]
    return (real_part.reshape(new_shape), imag_part.reshape(new_shape))


def sphere_coeffs(left_fields, right_fields, sphere_index, cosine, sine, cosine_x, sine_x):
    real_part, imag_part = pair_fields(left_fields, right_fields)
    real_part, imag_part = transform_axis(real_part, imag_part, cosine_x, sine_x, "pzyx,xk->pzyk")
    real_part, imag_part = transform_axis(real_part, imag_part, cosine, sine, "pzyk,yq->pzqk")
    spectra = jnp.stack([real_part, imag_part])
    wave_z = sphere_index // (NG * NX)
    wave_y = sphere_index // NX % NG
    wave_x = sphere_index % NX
    n_dev = lax.axis_size("grid")
    rows = NG // n_dev
    me_grid = lax.axis_index("grid")
    per_dev = NGV // n_dev
    slots = max(1, NGV // (n_dev * n_dev))
    source = wave_y // rows
    mine = (source == me_grid).reshape(n_dev, per_dev)
    rank = jnp.cumsum(mine.astype(jnp.int32), axis=1) - 1
    local_index = ((wave_z * rows + wave_y % rows) * NX + wave_x).reshape(n_dev, per_dev)
    match = mine[:, None, :] & (
        rank[:, None, :] == jnp.arange(slots, dtype=jnp.int32)[None, :, None]
    )
    chosen = jnp.sum(jnp.where(match, local_index[:, None, :], 0), axis=2).reshape(-1)
    filled = jnp.any(match, axis=2).reshape(-1).astype(jnp.float32)
    block = lax.all_to_all(spectra, "grid", split_axis=3, concat_axis=2, tiled=True)
    real_z, imag_z = transform_axis(block[0], block[1], cosine, sine, "pzyx,zq->pqyx")
    flat = jnp.stack([real_z, imag_z]).reshape(2, real_z.shape[0], -1)
    packed = jnp.take(flat, chosen, axis=2) * filled
    pairs = packed.shape[1]
    packed = packed.reshape(2, pairs, n_dev, slots)
    received = lax.all_to_all(packed, "grid", split_axis=2, concat_axis=2, tiled=True).reshape(
        2, pairs, n_dev * slots
    )
    own_source = lax.dynamic_slice_in_dim(source, me_grid * per_dev, per_dev)
    onehot = own_source[:, None] == jnp.arange(n_dev, dtype=jnp.int32)[None, :]
    running = jnp.cumsum(onehot.astype(jnp.int32), axis=0) - 1
    own_rank = jnp.sum(jnp.where(onehot, running, 0), axis=1)
    summed = jnp.take(received, own_source * slots + own_rank, axis=2)
    return summed * (1.0 / (NG * NG * NX) ** 0.5)


def local(left_bands, right_bands, sphere_index, right_order):
    cosine, sine = dft_tables(NG)
    cosine_x, sine_x = dft_tables(NX)
    own_left = left_bands.shape[1]
    own_right = right_bands.shape[1]
    other_right = swapped(right_bands, "band", 0)
    all_right = jnp.concatenate([right_bands, other_right], axis=1)
    coeffs = sphere_coeffs(left_bands, all_right, sphere_index, cosine, sine, cosine_x, sine_x)
    result = coeffs.reshape(2, own_left, 2 * own_right, -1)
    position = (right_order - lax.axis_index("band") * own_right) % right_order.shape[0]
    return jnp.take(result, position, axis=2)


def solution(mesh):
    placed = (P(None, "band", "grid", None, None), P(None, "band", "grid", None, None), P(), P())
    return jax.shard_map(
        local, mesh=mesh, in_specs=placed, out_specs=P(None, "band", None, "grid"), check_vma=False
    )
```

profile of v0, /device:TPU:1, one launch (start us, length us, event | category | flops | bytes accessed | tf_op | source)
XLA Modules:
  0.0 148.9 jit_solution(114899629044140723)
XLA Ops:
  0.0 2.1 %collective-permute-start = (f32[2,2,1,128,128]{4,3,2,1,0:T(8,128)}, f32[2,2,1,128,128]{4,3,2,1,0:T(8,128)S(1)}, u32[]{:S(2)}, u32[]{:S(2)}) collective-permute-start(f32[2,2,1,128,128]{4,3,2,1,0:T(8,128)} %param.5), channel_id=1, source_target_pairs={{0,1},{1,0},{2,3},{3,2},{4,5},{5,4},{6,7},{7,6},{8,9},{9,8},{10,11... | collective-permute-start | bytes 786440 | tf_op jit(solution)/shard_map/ppermute | solution.py:21
  4.2 3.1 %collective-permute-done = f32[2,2,1,128,128]{4,3,2,1,0:T(8,128)S(1)} collective-permute-done((f32[2,2,1,128,128]{4,3,2,1,0:T(8,128)}, f32[2,2,1,128,128]{4,3,2,1,0:T(8,128)S(1)}, u32[]{:S(2)}, u32[]{:S(2)}) %collective-permute-start) | collective-permute-done | bytes 262176 | tf_op jit(solution)/shard_map/ppermute | solution.py:21
  7.6 1.2 fusion.27
  8.9 1.2 fusion.25
  10.1 1.2 convolution_add_fusion.2
  11.3 1.3 fusion.29
  12.6 1.2 convolution_subtract_fusion.2
  13.9 1.3 fusion.23
  15.2 1.3 fusion.3
  16.5 1.3 fusion.2
  18.0 2.6 %copy.67 = f32[2,16,1,128,128]{4,1,2,0,3:T(8,128)} copy(f32[2,16,1,128,128]{4,3,1,2,0:T(8,128)S(1)} %pad_maximum_fusion) | data formatting | bytes 4194304 | tf_op jit(solution)/shard_map/stack | solution.py:57
  20.6 17.7 %all-to-all-start = ((f32[2,16,1,128,128]{4,1,2,0,3:T(8,128)}), f32[2,16,1,128,128]{4,1,2,0,3:T(8,128)S(1)}, u32[]{:S(2)}, u32[]{:S(2)}) async-start(f32[2,16,1,128,128]{4,1,2,0,3:T(8,128)} %copy.67), calls=%async_computation | async-start | bytes 4194304 | tf_op jit(solution)/shard_map/all_to_all | solution.py:75
  39.7 50.6 %all-to-all-done = f32[2,16,1,128,128]{4,1,2,0,3:T(8,128)S(1)} async-done(((f32[2,16,1,128,128]{4,1,2,0,3:T(8,128)}), f32[2,16,1,128,128]{4,1,2,0,3:T(8,128)S(1)}, u32[]{:S(2)}, u32[]{:S(2)}) %all-to-all-start) | async-done | bytes 2097184 | tf_op jit(solution)/shard_map/all_to_all | solution.py:75
  90.4 1.5 %fusion.4 = f32[128,16,128]{2,0,1:T(8,128)S(1)} fusion(f32[1,16,1,128,128]{4,1,2,0,3:T(8,128)S(1)} %get-tuple-element.14), kind=kOutput, calls=%fused_computation.19 | convolution fusion | flops 402882560 | bytes 2097152 | tf_op jit(solution)/shard_map/pzyx,zq->pqyx/dot_general | solution.py:35
  91.9 1.5 %fusion.5 = f32[128,16,128]{2,0,1:T(8,128)S(1)} fusion(f32[1,16,1,128,128]{4,1,2,0,3:T(8,128)S(1)} %get-tuple-element.15), kind=kOutput, calls=%fused_computation.20 | convolution fusion | flops 402882560 | bytes 2097152 | tf_op jit(solution)/shard_map/pzyx,zq->pqyx/dot_general | solution.py:36
  93.5 2.5 %fusion.1 = f32[16,128,1,128]{3,1,0,2:T(8,128)} fusion(f32[128,16,128]{2,0,1:T(8,128)S(1)} %fusion.4, f32[1,16,1,128,128]{4,1,2,0,3:T(8,128)S(1)} %get-tuple-element.15), kind=kOutput, calls=%fused_computation.8 | convolution fusion | flops 403144704 | bytes 3145728 | tf_op jit(solution)/shard_map/pzyx,zq->pqyx/dot_general | solution.py:35
  96.0 2.4 %stack.21 = f32[1,16,16384]{2,1,0:T(8,128)} reshape(f32[16,128,1,128]{3,1,0,2:T(8,128)} %fusion.1) | data formatting | bytes 2097152 | tf_op jit(solution)/shard_map/stack | solution.py:77
  98.4 1.5 %fusion = f32[16,128,1,128]{3,1,0,2:T(8,128)S(1)} fusion(f32[128,16,128]{2,0,1:T(8,128)S(1)} %fusion.5, f32[1,16,1,128,128]{4,1,2,0,3:T(8,128)S(1)} %get-tuple-element.14), kind=kOutput, calls=%fused_computation.6 | convolution fusion | flops 403144704 | bytes 3145728 | tf_op jit(solution)/shard_map/pzyx,zq->pqyx/dot_general | solution.py:36
  99.9 1.2 stack.22
  101.3 1.4 pad_maximum_fusion.1
  102.7 14.9 %copy.74 = f32[2,16,16384]{1,0,2:T(2,128)} copy(f32[2,16,16384]{2,1,0:T(8,128)S(1)} %pad_maximum_fusion.1) | data formatting | bytes 4194304 | tf_op jit(solution)/shard_map/stack | solution.py:77
  117.6 6.5 %gather_fusion = f32[128,2,16]{2,1,0:T(2,128)S(1)} fusion(f32[2,16,16384]{1,0,2:T(2,128)} %copy.74, s32[1024]{0:T(1024)S(1)} %get-tuple-element.23), kind=kCustom, calls=%fused_computation | custom fusion | bytes 33280 | tf_op jit(solution)/shard_map/jit(_take)/gather | solution.py:78
  125.0 8.2 %all-to-all-start.1 = ((f32[2,16,128,1]{1,0,3,2:T(2,128)}), f32[2,16,128,1]{1,0,3,2:T(2,128)S(1)}, u32[]{:S(2)}, u32[]{:S(2)}) async-start(f32[2,16,128,1]{1,0,3,2:T(2,128)} %copy.76), calls=%async_computation.1 | async-start | bytes 262144 | tf_op jit(solution)/shard_map/all_to_all | solution.py:81
  133.2 13.6 %all-to-all-done.1 = f32[2,16,128,1]{1,0,3,2:T(2,128)S(1)} async-done(((f32[2,16,128,1]{1,0,3,2:T(2,128)}), f32[2,16,128,1]{1,0,3,2:T(2,128)S(1)}, u32[]{:S(2)}, u32[]{:S(2)}) %all-to-all-start.1) | async-done | bytes 16416 | tf_op jit(solution)/shard_map/all_to_all | solution.py:81
  (39 shorter events, 7.3 us)
Async XLA Ops:
  0.0 7.3 %collective-permute-start = (f32[2,2,1,128,128]{4,3,2,1,0:T(8,128)}, f32[2,2,1,128,128]{4,3,2,1,0:T(8,128)S(1)}, u32[]{:S(2)}, u32[]{:S(2)}) collective-permute-start(f32[2,2,1,128,128]{4,3,2,1,0:T(8,128)} %param.5), channel_id=1, source_target_pairs={{0,1},{1,0},{2,3},{3,2},{4,5},{5,4},{6,7},{7,6},{8,9},{9,8},{10,11... | collective-permute-start | bytes 786440 | tf_op jit(solution)/shard_map/ppermute | solution.py:21
  20.6 17.7 %copy-start.1 = (s32[16384]{0:T(1024)S(1)}, s32[16384]{0:T(1024)}, u32[]{:S(2)}) copy-start(s32[16384]{0:T(1024)} %param.6) | copy-start | bytes 196612
  20.6 18.8 %copy-start.2 = (s32[4]{0:T(128)S(1)}, s32[4]{0:T(128)}, u32[]{:S(2)}) copy-start(s32[4]{0:T(128)} %param.7) | copy-start | bytes 52
  20.6 69.7 %all-to-all-start = ((f32[2,16,1,128,128]{4,1,2,0,3:T(8,128)}), f32[2,16,1,128,128]{4,1,2,0,3:T(8,128)S(1)}, u32[]{:S(2)}, u32[]{:S(2)}) async-start(f32[2,16,1,128,128]{4,1,2,0,3:T(8,128)} %copy.67), calls=%async_computation | async-start | bytes 4194304 | tf_op jit(solution)/shard_map/all_to_all | solution.py:75
  99.9 1.5 copy-start
  125.0 21.8 %all-to-all-start.1 = ((f32[2,16,128,1]{1,0,3,2:T(2,128)}), f32[2,16,128,1]{1,0,3,2:T(2,128)S(1)}, u32[]{:S(2)}, u32[]{:S(2)}) async-start(f32[2,16,128,1]{1,0,3,2:T(2,128)} %copy.76), calls=%async_computation.1 | async-start | bytes 262144 | tf_op jit(solution)/shard_map/all_to_all | solution.py:81
where the time goes:
time: 149 us
  waiting for transfers between devices  67.3 us (45%)
  local copies, waits for them, and re-layouts  33.2 us (22%)
  starting transfers between devices  28 us (19%)
  matrix products  17.1 us (11%)
  other arithmetic  3.04 us (2%)
    all_to_all x1, waiting for transfers between devices, sphere_coeffs(): lax.all_to_all(spectra, 'grid', split_axis=3, concat_axis=2, tiled=True)  50.6 us
    another operation x3, local copies, waits for them, and re-layouts, sphere_coeffs(): flat = jnp.stack([real_z, imag_z]).reshape(2, real_z.shape[0], -1)  18.5 us
    all_to_all x1, starting transfers between devices, sphere_coeffs(): lax.all_to_all(spectra, 'grid', split_axis=3, concat_axis=2, tiled=True)  17.7 us
    all_to_all x1, waiting for transfers between devices, sphere_coeffs(): lax.all_to_all(packed, 'grid', split_axis=2, concat_axis=2, tiled=True)  13.6 us
    all_to_all x1, starting transfers between devices, sphere_coeffs(): lax.all_to_all(packed, 'grid', split_axis=2, concat_axis=2, tiled=True)  8.17 us
    gather x2, local copies, waits for them, and re-layouts, sphere_coeffs(): packed = jnp.take(flat, chosen, axis=2) * filled  6.58 us
    dot_general x3, matrix products, transform_axis(): product(imag_part, sine)  5.07 us
    dot_general x3, matrix products, transform_axis(): product(real_part, sine)  4.05 us
  transfers between devices with their start and end apart: 3, of which 3 were waited for; matrix products, arithmetic and copies ran while one was open for 2% of the time, Pallas kernels for 0%

commit v1 on v0

v1 whole, which is shorter than its diff:
```python
import functools
import math

import jax
import jax.numpy as jnp
from jax import lax
from jax.experimental import pallas as pl
from jax.experimental.pallas import tpu as pltpu
from jax.sharding import PartitionSpec as P
import numpy as np

NG = 128
NX = 128
NGV = 16384
AX, AH, AZ, AC = 4, 2, 8, 2
SIDE = AH * AZ * AC
QUARTER = SIDE * 8
HALF = QUARTER // 2
MESH = pl.DeviceIdType.MESH
F32 = jnp.float32
BF16 = jnp.bfloat16


def split(value):
    high = value.astype(BF16)
    return high, (value - high.astype(F32)).astype(BF16)


def dft_tables():
    counter = np.arange(NG)
    angles = (counter[:, None] * counter[None, :] % NG) * (2.0 * math.pi / NG)
    cosine, sine = np.cos(angles), np.sin(angles)

    def halves(table):
        high = table.astype(np.float32).astype(BF16)
        low = (table - high.astype(np.float64)).astype(np.float32).astype(BF16)
        return high, low

    high, low = halves(np.block([[cosine, -sine], [sine, cosine]]))
    along_x = np.concatenate([high, high, low], axis=0)
    high, low = halves(np.block([[cosine, sine], [-sine, cosine]]))
    along_y = np.concatenate([high, low, high], axis=1)
    trig = np.zeros((8, NG), np.float32)
    trig[0], trig[1] = cosine[1], sine[1]
    return along_x, along_y, trig


def lanes(value, index):
    return jnp.take_along_axis(value, index, axis=1, mode="promise_in_bounds")


def kernel(
    left_ref, right_ref, sphere_ref, along_x_ref, along_y_ref, trig_ref, out_ref, row_ref,
    lefts, rights, own_right, sphere, along_x, along_y, trig,
    ky_t, val_t, kx_of, phase, acc, send, from_a, from_b, from_c, x_sum, tiles,
    load_sem, pair_send, pair_recv, y_send, y_recv, x_send, x_recv, z_send, z_recv,
):
    g = lax.axis_index("grid")
    b = lax.axis_index("band")
    c = lax.rem(g, AC)
    j = lax.rem(g, SIDE)
    x = lax.div(g, SIDE)
    up = lax.rem(x + 1, AX)
    down = lax.rem(x + AX - 1, AX)
    across = lax.rem(x + 2, AX)

    loads = [
        pltpu.make_async_copy(sphere_ref, sphere, load_sem.at[0]),
        pltpu.make_async_copy(trig_ref, trig, load_sem.at[1]),
        pltpu.make_async_copy(right_ref, own_right, load_sem.at[2]),
        pltpu.make_async_copy(left_ref, lefts.at[c], load_sem.at[3]),
        pltpu.make_async_copy(right_ref.at[:, c], rights.at[0, c], load_sem.at[4]),
        pltpu.make_async_copy(along_x_ref, along_x, load_sem.at[5]),
        pltpu.make_async_copy(along_y_ref, along_y, load_sem.at[6]),
    ]
    for load in loads:
        load.start()

    barrier = pltpu.get_barrier_semaphore()

    def greet(grid, band):
        pl.semaphore_signal(barrier, inc=1, device_id=(grid, band), device_id_type=MESH)

    greet(g - c, 1 - b)
    greet(g - c + 1, 1 - b)
    greet(up * SIDE + j, b)
    greet(down * SIDE + j, b)

    @pl.loop(1, SIDE)
    def _(step):
        greet(x * SIDE + lax.rem(j + step, SIDE), b)

    loads[0].wait()
    loads[1].wait()
    flipped = sphere[...].T
    ky_t[...] = (flipped >> 7) & 127
    val_t[...] = ((flipped >> 14) << 7) | (flipped & 127)
    rows = lax.broadcasted_iota(jnp.int32, (NG, NG), 0)

    def place(p, table):
        return jnp.where(ky_t[pl.ds(p, 1), :] == rows, val_t[pl.ds(p, 1), :], table)

    table = lax.fori_loop(0, NG, place, jnp.zeros((NG, NG), jnp.int32), unroll=8)
    kx_of[...] = table & 127
    kz = table >> 7
    cosine = jnp.broadcast_to(trig[0:1, :], (NG, NG))
    sine = jnp.broadcast_to(trig[1:2, :], (NG, NG))
    for core in range(2):
        angle = (kz * (g - c + core)) & 127
        phase[core, 0] = lanes(cosine, angle)
        phase[core, 1] = lanes(sine, angle)
    row_ref[...] = jnp.broadcast_to((sphere[pl.ds(g, 1), :] >> 7) & 127, (8, NG))

    def transform(chunk, plane, combine):
        right_real = rights[chunk, plane, 0]
        right_imag = rights[chunk, plane, 1]
        index = kx_of[...]
        for half in range(2):
            columns = []
            for n in (2 * half, 2 * half + 1):
                left_real = lefts[plane, 0, n]
                left_imag = lefts[plane, 1, n]
                field = jnp.concatenate(
                    [
                        left_real * right_real + left_imag * right_imag,
                        left_real * right_imag - left_imag * right_real,
                    ],
                    axis=1,
                )
                high, low = split(field)
                moved = jnp.dot(
                    jnp.concatenate([high, low, high], axis=1),
                    along_x[...],
                    preferred_element_type=F32,
                )
                columns.append(jnp.concatenate([moved[:, :NX], moved[:, NX:]], axis=0))
            high, low = split(jnp.concatenate(columns, axis=1))
            plane_waves = jnp.dot(
                along_y[...],
                jnp.concatenate([high, high, low], axis=0),
                preferred_element_type=F32,
            )
            for at, n in enumerate((2 * half, 2 * half + 1)):
                real = lanes(plane_waves[:NG, at * NX : (at + 1) * NX], index)
                imag = lanes(plane_waves[NG:, at * NX : (at + 1) * NX], index)
                cosines, sines = phase[plane, 0], phase[plane, 1]
                combine(n, real * cosines + imag * sines)
                combine(n + 4, imag * cosines - real * sines)

    def keep(channel, value):
        acc[channel] = value

    def finish(chunk, channel, value):
        send[chunk, pl.ds(channel, NG, stride=8), :] = (acc[channel] + value).T

    for load in loads[2:]:
        load.wait()
    transform(0, c, keep)

    pl.semaphore_wait(barrier, SIDE - 1 + 4)

    def remote(source, target, sent, received, grid, band):
        return pltpu.make_async_remote_copy(
            src_ref=source, dst_ref=target, send_sem=sent, recv_sem=received,
            device_id=(grid, band), device_id_type=MESH,
        )

    to_other = [
        remote(own_right.at[:, m], rights.at[1, c], y_send.at[m], y_recv.at[c], g - c + m, 1 - b)
        for m in range(2)
    ]
    pair = g + 1 - 2 * c
    to_pair = [
        remote(lefts.at[c], lefts.at[c], pair_send.at[0], pair_recv.at[0], pair, b),
        remote(own_right.at[:, 1 - c], rights.at[0, c], pair_send.at[1], pair_recv.at[1], pair, b),
    ]
    for copy in to_pair + to_other:
        copy.start()
    for copy in to_pair:
        copy.wait_recv()
    transform(0, 1 - c, functools.partial(finish, 0))

    def part(chunk, quarter, half):
        start = pl.multiple_of(quarter * QUARTER + half * HALF, HALF)
        return send.at[chunk, pl.ds(start, HALF)]

    grid_up = up * SIDE + j
    grid_down = down * SIDE + j

    def x_copies(chunk):
        sent, received = x_send.at[chunk], x_recv.at[chunk]
        return [
            remote(part(chunk, across, 0), from_a.at[chunk, 0], sent.at[0], received.at[0], grid_up, b),
            remote(part(chunk, across, 1), from_a.at[chunk, 1], sent.at[1], received.at[1], grid_down, b),
            remote(part(chunk, up, 1), from_b.at[chunk, 0], sent.at[2], received.at[2], grid_up, b),
            remote(part(chunk, down, 0), from_b.at[chunk, 1], sent.at[3], received.at[3], grid_down, b),
            remote(part(chunk, up, 0), from_c.at[chunk, 0], sent.at[4], received.at[4], grid_up, b),
            remote(part(chunk, down, 1), from_c.at[chunk, 1], sent.at[5], received.at[5], grid_down, b),
        ]

    def x_first(copies):
        for copy in copies[:4]:
            copy.start()

    def x_second(chunk, copies):
        for way, quarter in enumerate((up, down)):
            copies[way].wait_recv()
            ref = part(chunk, quarter, way)
            ref[...] = ref[...] + from_a[chunk, way]
            copies[4 + way].start()

    def z_first(chunk, copies):
        for copy in copies[2:]:
            copy.wait_recv()
        for half in range(2):
            x_sum[chunk, pl.ds(half * HALF, HALF)] = (
                part(chunk, x, half)[...] + from_c[chunk, half] + from_b[chunk, 1 - half]
            )
        mine = pl.ds(pl.multiple_of(j * 8, 8), 8)
        tiles[chunk, mine] = x_sum[chunk, mine]

        @pl.loop(1, SIDE)
        def _(step):
            to = lax.rem(j + step, SIDE)
            theirs = pl.ds(pl.multiple_of(to * 8, 8), 8)
            remote(
                x_sum.at[chunk, theirs], tiles.at[chunk, mine],
                z_send.at[chunk], z_recv.at[chunk], x * SIDE + to, b,
            ).start()

    def z_wait(buffer, chunk, sem):
        many = buffer.at[chunk, pl.ds(0, (SIDE - 1) * 8)]
        pltpu.make_async_copy(many, many, sem.at[chunk]).wait()

    def z_last(chunk):
        z_wait(tiles, chunk, z_recv)
        for core in range(2):
            total = tiles[chunk, pl.ds(core * 8, 8)]
            for chip in range(1, SIDE // 2):
                total = total + tiles[chunk, pl.ds((2 * chip + core) * 8, 8)]
            out_ref[pl.ds((2 * chunk + core) * 8, 8), :] = total

    native = x_copies(0)
    distant = x_copies(1)
    x_first(native)
    x_second(0, native)

    def arrival(core):
        return remote(
            own_right.at[:, 0], rights.at[1, core], y_send.at[0], y_recv.at[core], g, 1 - b
        )

    arrival(0).wait_recv()
    transform(1, 0, keep)
    arrival(1).wait_recv()
    transform(1, 1, functools.partial(finish, 1))
    x_first(distant)
    z_first(0, native)
    x_second(1, distant)
    z_first(1, distant)
    z_last(0)
    z_last(1)

    for copy in to_pair + to_other + native + distant:
        copy.wait_send()
    for chunk in range(2):
        z_wait(x_sum, chunk, z_send)


def last_kernel(order_ref, sums_ref, row_ref, out_ref):
    index = row_ref[...]
    factor = 1.0 / (NG * NG * NX) ** 0.5
    for column in range(4):
        start = pl.multiple_of(order_ref[column] * 8, 8)
        value = lanes(sums_ref[pl.ds(start, 8), :], index) * factor
        out_ref[pl.ds(column, 8, stride=4), :] = value


def local(left_bands, right_bands, sphere_index, right_order):
    along_x, along_y, trig = dft_tables()
    hbm = pl.BlockSpec(memory_space=pltpu.HBM)
    vmem = pl.BlockSpec(memory_space=pltpu.VMEM)
    dma = pltpu.SemaphoreType.DMA
    sums, row = pl.pallas_call(
        kernel,
        name="pair_sums",
        out_shape=(
            jax.ShapeDtypeStruct((32, NG), F32),
            jax.ShapeDtypeStruct((8, NG), jnp.int32),
        ),
        in_specs=[hbm] * 6,
        out_specs=(vmem, vmem),
        scratch_shapes=[
            pltpu.VMEM((2, 2, 4, NG, NX), F32),
            pltpu.VMEM((2, 2, 2, NG, NX), F32),
            pltpu.VMEM((2, 2, NG, NX), F32),
            pltpu.VMEM((NG, NG), jnp.int32),
            pltpu.VMEM((6 * NG, 2 * NG), BF16),
            pltpu.VMEM((2 * NG, 6 * NG), BF16),
            pltpu.VMEM((8, NG), F32),
            pltpu.VMEM((NG, NG), jnp.int32),
            pltpu.VMEM((NG, NG), jnp.int32),
            pltpu.VMEM((NG, NG), jnp.int32),
            pltpu.VMEM((2, 2, NG, NG), F32),
            pltpu.VMEM((8, NG, NG), F32),
            pltpu.VMEM((2, AX * QUARTER, NG), F32),
            pltpu.VMEM((2, 2, HALF, NG), F32),
            pltpu.VMEM((2, 2, HALF, NG), F32),
            pltpu.VMEM((2, 2, HALF, NG), F32),
            pltpu.VMEM((2, QUARTER, NG), F32),
            pltpu.VMEM((2, QUARTER, NG), F32),
            dma((7,)), dma((2,)), dma((2,)), dma((2,)), dma((2,)),
            dma((2, 6)), dma((2, 6)), dma((2,)), dma((2,)),
        ],
        compiler_params=pltpu.CompilerParams(collective_id=0, has_side_effects=True),
    )(
        left_bands.reshape(2, 4, NG, NX),
        right_bands.reshape(2, 2, NG, NX),
        sphere_index.reshape(NG, NG),
        jnp.asarray(along_x),
        jnp.asarray(along_y),
        jnp.asarray(trig),
    )
    position = (right_order - lax.axis_index("band") * 2) % 4
    result = pl.pallas_call(
        last_kernel,
        name="place",
        out_shape=jax.ShapeDtypeStruct((32, NG), F32),
        in_specs=[pl.BlockSpec(memory_space=pltpu.SMEM), vmem, vmem],
        out_specs=vmem,
    )(position, sums, row)
    return result.reshape(2, 4, 4, NG)


def solution(mesh):
    placed = (P(None, "band", "grid", None, None), P(None, "band", "grid", None, None), P(), P())
    return jax.shard_map(
        local, mesh=mesh, in_specs=placed, out_specs=P(None, "band", None, "grid"), check_vma=False
    )
```

time: 149 us -> 38 us (0.26)
  waiting for transfers between devices: 67.3 us -> 0 us
  Pallas kernels: 0 us -> 36.7 us
  local copies, waits for them, and re-layouts: 33.2 us -> 0.65 us
  starting transfers between devices: 28 us -> 0 us
  matrix products: 17.1 us -> 0 us
  other arithmetic: 3.04 us -> 0.55 us
    all_to_all x2 -> x0, waiting for transfers between devices: 64.2 us -> none  [the longest x1 50.6 us: sphere_coeffs(): lax.all_to_all(spectra, 'grid', split_axis=3, concat_axis=2, tiled=True)]
    pallas_call x0 -> x2, Pallas kernels: none -> 36.7 us  [the longest x1 35.3 us: local(): pl.pallas_call(kernel, name='pair_sums', out_shape=(jax.ShapeDtypeStruct(...]
    all_to_all x2 -> x0, starting transfers between devices: 25.8 us -> none  [the longest x1 17.7 us: sphere_coeffs(): lax.all_to_all(spectra, 'grid', split_axis=3, concat_axis=2, tiled=True)]
    another operation x5 -> x0, local copies, waits for them, and re-layouts: 21.2 us -> none  [the longest x3 18.5 us: sphere_coeffs(): flat = jnp.stack([real_z, imag_z]).reshape(2, real_z.shape[0], -1)]
    dot_general x12 -> x0, matrix products: 17.1 us -> none  [the longest x3 5.07 us: transform_axis(): product(imag_part, sine)]
    gather x5 -> x0, local copies, waits for them, and re-layouts: 7.96 us -> none  [the longest x2 6.58 us: sphere_coeffs(): packed = jnp.take(flat, chosen, axis=2) * filled]
    ppermute x1 -> x0, waiting for transfers between devices: 3.09 us -> none  [swapped(): return lax.ppermute(block, axis, route)]
    ppermute x1 -> x0, starting transfers between devices: 2.11 us -> none  [swapped(): return lax.ppermute(block, axis, route)]
  transfers between devices with their start and end apart: 3 -> 0, of which waited for: 3 -> 0; matrix products, arithmetic and copies ran while one was open for 2% -> 0% of each run, Pallas kernels for 0% -> 0%
where the time goes in v1:
time: 38 us; the launch traced here: 37.9 us
  Pallas kernels  36.7 us (97%)
  local copies, waits for them, and re-layouts  0.65 us (2%)
  other arithmetic  0.55 us (1%)
    pallas_call x1, Pallas kernels, local(): pl.pallas_call(kernel, name='pair_sums', out_shape=(jax.ShapeDtypeStruct(...  35.3 us
    pallas_call x1, Pallas kernels, local(): pl.pallas_call(last_kernel, name='place', out_shape=jax.ShapeDtypeStruct(...  1.41 us

profile of v1, /device:TPU:1, one launch (start us, length us, event | category | flops | bytes accessed | tf_op | source)
XLA Modules:
  0.0 37.9 jit_solution(5985325691827543280)
XLA Ops:
  0.0 0.0 copy-start
  0.0 0.7 %copy-done = s32[4]{0:T(128)S(1)} copy-done((s32[4]{0:T(128)S(1)}, s32[4]{0:T(128)}, u32[]{:S(2)}) %copy-start) | copy-done | bytes 40
  0.7 0.5 %and_select_fusion.order_ref = s32[4]{0:T(128)} fusion(s32[4]{0:T(128)S(1)} %copy-done, s32[]{:T(128)S(6)} %mul.3), kind=kLoop, calls=%fused_computation.2 | loop fusion | flops 48 | bytes 36 | tf_op jit(solution)/shard_map/jit(remainder)/select_n | solution.py:324
  1.2 35.3 %pair_sums.1 = (f32[32,128]{1,0:T(8,128)}, s32[8,128]{1,0:T(8,128)}) custom-call(f32[2,4,128,128]{3,2,1,0:T(8,128)} %bitcast.4, f32[2,2,128,128]{3,2,1,0:T(8,128)} %bitcast.5, s32[128,128]{1,0:T(8,128)} %bitcast.6, bf16[768,256]{1,0:T(8,128)(2,1)} %constant.27.clone.along_x_ref, bf16[256,768]{1,0:T(8,128)(2,1)} %constant.28.clone.along_y_ref, ...), custom_call_target="tpu_custom_call" | custom-call | tf_op jit(solution)/shard_map/pair_sums/pallas_call | solution.py:284
  36.5 1.4 %place.1 = f32[32,128]{1,0:T(8,128)} custom-call(s32[4]{0:T(128)} %and_select_fusion.order_ref, f32[32,128]{1,0:T(8,128)} %get-tuple-element.7.sums_ref, s32[8,128]{1,0:T(8,128)} %get-tuple-element.8.row_ref), custom_call_target="tpu_custom_call" | custom-call | tf_op jit(solution)/shard_map/place/pallas_call | solution.py:325
Async XLA Ops:
  0.0 0.7 %copy-start = (s32[4]{0:T(128)S(1)}, s32[4]{0:T(128)}, u32[]{:S(2)}) copy-start(s32[4]{0:T(128)} %param.10) | copy-start | bytes 52

commit v2 on v1

--- a/solution.py
+++ b/solution.py
@@ -50,10 +50,10 @@
 
 
 def kernel(
-    left_ref, right_ref, sphere_ref, along_x_ref, along_y_ref, trig_ref, out_ref, row_ref,
+    order_ref, left_ref, right_ref, sphere_ref, along_x_ref, along_y_ref, trig_ref, out_ref,
     lefts, rights, own_right, sphere, along_x, along_y, trig,
     ky_t, val_t, kx_of, phase, acc, send, from_a, from_b, from_c, x_sum, tiles,
-    load_sem, pair_send, pair_recv, y_send, y_recv, x_send, x_recv, z_send, z_recv,
+    load_sem, pair_send, pair_recv, y_send, y_recv, x_send, x_recv, z_send, z_recv, known,
 ):
     g = lax.axis_index("grid")
     b = lax.axis_index("band")
@@ -65,10 +65,10 @@
     across = lax.rem(x + 2, AX)
 
     loads = [
-        pltpu.make_async_copy(sphere_ref, sphere, load_sem.at[0]),
-        pltpu.make_async_copy(trig_ref, trig, load_sem.at[1]),
-        pltpu.make_async_copy(right_ref, own_right, load_sem.at[2]),
-        pltpu.make_async_copy(left_ref, lefts.at[c], load_sem.at[3]),
+        pltpu.make_async_copy(right_ref, own_right, load_sem.at[0]),
+        pltpu.make_async_copy(left_ref, lefts.at[c], load_sem.at[1]),
+        pltpu.make_async_copy(sphere_ref, sphere, load_sem.at[2]),
+        pltpu.make_async_copy(trig_ref, trig, load_sem.at[3]),
         pltpu.make_async_copy(right_ref.at[:, c], rights.at[0, c], load_sem.at[4]),
         pltpu.make_async_copy(along_x_ref, along_x, load_sem.at[5]),
         pltpu.make_async_copy(along_y_ref, along_y, load_sem.at[6]),
@@ -76,22 +76,61 @@
     for load in loads:
         load.start()
 
+    grid_up = up * SIDE + j
+    grid_down = down * SIDE + j
+    pair = g + 1 - 2 * c
+    z = lax.rem(lax.div(g, AC), AZ)
+    opposite = g + SIDE // 2 - SIDE * lax.rem(lax.div(g, SIDE // 2), AH)
+    along_z = [g + AC * (lax.rem(z + step, AZ) - z) for step in (1, 2, AZ - 1, AZ - 2)]
+    friends = along_z + [opposite, pair]
     barrier = pltpu.get_barrier_semaphore()
 
-    def greet(grid, band):
-        pl.semaphore_signal(barrier, inc=1, device_id=(grid, band), device_id_type=MESH)
-
-    greet(g - c, 1 - b)
-    greet(g - c + 1, 1 - b)
-    greet(up * SIDE + j, b)
-    greet(down * SIDE + j, b)
-
-    @pl.loop(1, SIDE)
-    def _(step):
-        greet(x * SIDE + lax.rem(j + step, SIDE), b)
-
+    def signal(sem, grid, band):
+        pl.semaphore_signal(sem, inc=1, device_id=(grid, band), device_id_type=MESH)
+
+    signal(barrier, g - c, 1 - b)
+    signal(barrier, g - c + 1, 1 - b)
+    signal(barrier, grid_up, b)
+    signal(barrier, grid_down, b)
+    for friend in friends:
+        signal(barrier, friend, b)
+
+    def tell(step):
+        for friend in friends:
+            signal(known.at[step], friend, b)
+
+    def hear(step):
+        pl.semaphore_wait(known.at[step], len(friends))
+
+    def remote(source, target, sent, received, grid, band):
+        return pltpu.make_async_remote_copy(
+            src_ref=source, dst_ref=target, send_sem=sent, recv_sem=received,
+            device_id=(grid, band), device_id_type=MESH,
+        )
+
+    to_other = [
+        remote(own_right.at[:, m], rights.at[1, c], y_send.at[m], y_recv.at[c], g - c + m, 1 - b)
+        for m in range(2)
+    ]
+    to_pair = [
+        remote(lefts.at[c], lefts.at[c], pair_send.at[0], pair_recv.at[0], pair, b),
+        remote(own_right.at[:, 1 - c], rights.at[0, c], pair_send.at[1], pair_recv.at[1], pair, b),
+    ]
     loads[0].wait()
     loads[1].wait()
+    pl.semaphore_wait(barrier, 4 + len(friends))
+
+    @pl.when(c == 0)
+    def _():
+        for copy in to_other:
+            copy.start()
+
+    for copy in to_pair:
+        copy.start()
+    tell(0)
+
+    loads[2].wait()
+    loads[3].wait()
     flipped = sphere[...].T
     ky_t[...] = (flipped >> 7) & 127
     val_t[...] = ((flipped >> 14) << 7) | (flipped & 127)
@@ -109,7 +148,11 @@
         angle = (kz * (g - c + core)) & 127
         phase[core, 0] = lanes(cosine, angle)
         phase[core, 1] = lanes(sine, angle)
-    row_ref[...] = jnp.broadcast_to((sphere[pl.ds(g, 1), :] >> 7) & 127, (8, NG))
+
+    @pl.when(c == 1)
+    def _():
+        for copy in to_other:
+            copy.start()
 
     def transform(chunk, plane, combine):
         right_real = rights[chunk, plane, 0]
@@ -153,29 +196,11 @@
     def finish(chunk, channel, value):
         send[chunk, pl.ds(channel, NG, stride=8), :] = (acc[channel] + value).T
 
-    for load in loads[2:]:
+    for load in loads[4:]:
         load.wait()
     transform(0, c, keep)
-
-    pl.semaphore_wait(barrier, SIDE - 1 + 4)
-
-    def remote(source, target, sent, received, grid, band):
-        return pltpu.make_async_remote_copy(
-            src_ref=source, dst_ref=target, send_sem=sent, recv_sem=received,
-            device_id=(grid, band), device_id_type=MESH,
-        )
-
-    to_other = [
-        remote(own_right.at[:, m], rights.at[1, c], y_send.at[m], y_recv.at[c], g - c + m, 1 - b)
-        for m in range(2)
-    ]
-    pair = g + 1 - 2 * c
-    to_pair = [
-        remote(lefts.at[c], lefts.at[c], pair_send.at[0], pair_recv.at[0], pair, b),
-        remote(own_right.at[:, 1 - c], rights.at[0, c], pair_send.at[1], pair_recv.at[1], pair, b),
-    ]
-    for copy in to_pair + to_other:
-        copy.start()
+    hear(0)
+    tell(1)
     for copy in to_pair:
         copy.wait_recv()
     transform(0, 1 - c, functools.partial(finish, 0))
@@ -183,9 +208,6 @@
     def part(chunk, quarter, half):
         start = pl.multiple_of(quarter * QUARTER + half * HALF, HALF)
         return send.at[chunk, pl.ds(start, HALF)]
-
-    grid_up = up * SIDE + j
-    grid_down = down * SIDE + j
 
     def x_copies(chunk):
         sent, received = x_send.at[chunk], x_recv.at[chunk]
@@ -232,18 +254,24 @@
         many = buffer.at[chunk, pl.ds(0, (SIDE - 1) * 8)]
         pltpu.make_async_copy(many, many, sem.at[chunk]).wait()
 
+    index = jnp.broadcast_to((sphere[pl.ds(g, 1), :] >> 7) & 127, (8, NG))
+    factor = 1.0 / (NG * NG * NX) ** 0.5
+
     def z_last(chunk):
         z_wait(tiles, chunk, z_recv)
+        values = []
         for core in range(2):
             total = tiles[chunk, pl.ds(core * 8, 8)]
             for chip in range(1, SIDE // 2):
                 total = total + tiles[chunk, pl.ds((2 * chip + core) * 8, 8)]
-            out_ref[pl.ds((2 * chunk + core) * 8, 8), :] = total
+            values.append(lanes(total, index) * factor)
+        return values
 
     native = x_copies(0)
     distant = x_copies(1)
     x_first(native)
-    x_second(0, native)
+    hear(1)
+    tell(2)
 
     def arrival(core):
         return remote(
@@ -255,11 +283,19 @@
     arrival(1).wait_recv()
     transform(1, 1, functools.partial(finish, 1))
     x_first(distant)
+    x_second(0, native)
+    hear(2)
+    x_second(1, distant)
     z_first(0, native)
-    x_second(1, distant)
     z_first(1, distant)
-    z_last(0)
-    z_last(1)
+    values = z_last(0)
+    values = values + z_last(1)
+    for column in range(4):
+        position = jnp.full((8, NG), lax.rem(order_ref[column] + 4 - 2 * b, 4), jnp.int32)
+        value = values[3]
+        for at in range(3):
+            value = jnp.where(position == at, values[at], value)
+        out_ref[pl.ds(column, 8, stride=4), :] = value
 
     for copy in to_pair + to_other + native + distant:
         copy.wait_send()
@@ -267,29 +303,16 @@
         z_wait(x_sum, chunk, z_send)
 
 
-def last_kernel(order_ref, sums_ref, row_ref, out_ref):
-    index = row_ref[...]
-    factor = 1.0 / (NG * NG * NX) ** 0.5
-    for column in range(4):
-        start = pl.multiple_of(order_ref[column] * 8, 8)
-        value = lanes(sums_ref[pl.ds(start, 8), :], index) * factor
-        out_ref[pl.ds(column, 8, stride=4), :] = value
-
-
 def local(left_bands, right_bands, sphere_index, right_order):
     along_x, along_y, trig = dft_tables()
     hbm = pl.BlockSpec(memory_space=pltpu.HBM)
-    vmem = pl.BlockSpec(memory_space=pltpu.VMEM)
     dma = pltpu.SemaphoreType.DMA
-    sums, row = pl.pallas_call(
+    result = pl.pallas_call(
         kernel,
         name="pair_sums",
-        out_shape=(
-            jax.ShapeDtypeStruct((32, NG), F32),
-            jax.ShapeDtypeStruct((8, NG), jnp.int32),
-        ),
-        in_specs=[hbm] * 6,
-        out_specs=(vmem, vmem),
+        out_shape=jax.ShapeDtypeStruct((32, NG), F32),
+        in_specs=[pl.BlockSpec(memory_space=pltpu.SMEM)] + [hbm] * 6,
+        out_specs=pl.BlockSpec(memory_space=pltpu.VMEM),
         scratch_shapes=[
             pltpu.VMEM((2, 2, 4, NG, NX), F32),
             pltpu.VMEM((2, 2, 2, NG, NX), F32),
@@ -310,10 +333,11 @@
             pltpu.VMEM((2, QUARTER, NG), F32),
             pltpu.VMEM((2, QUARTER, NG), F32),
             dma((7,)), dma((2,)), dma((2,)), dma((2,)), dma((2,)),
-            dma((2, 6)), dma((2, 6)), dma((2,)), dma((2,)),
+            dma((2, 6)), dma((2, 6)), dma((2,)), dma((2,)), pltpu.SemaphoreType.REGULAR((3,)),
         ],
         compiler_params=pltpu.CompilerParams(collective_id=0, has_side_effects=True),
     )(
+        right_order,
         left_bands.reshape(2, 4, NG, NX),
         right_bands.reshape(2, 2, NG, NX),
         sphere_index.reshape(NG, NG),
@@ -321,14 +345,6 @@
         jnp.asarray(along_y),
         jnp.asarray(trig),
     )
-    position = (right_order - lax.axis_index("band") * 2) % 4
-    result = pl.pallas_call(
-        last_kernel,
-        name="place",
-        out_shape=jax.ShapeDtypeStruct((32, NG), F32),
-        in_specs=[pl.BlockSpec(memory_space=pltpu.SMEM), vmem, vmem],
-        out_specs=vmem,
-    )(position, sums, row)
     return result.reshape(2, 4, 4, NG)
 
 

time: 38 us -> 36.8 us (0.968)
  Pallas kernels: 36.7 us -> 35.3 us
  local copies, waits for them, and re-layouts: 0.65 us -> 1.32 us
  other arithmetic: 0.55 us -> 0 us
    pallas_call x2 -> x1, Pallas kernels: 36.7 us -> 35.3 us  [local(): pl.pallas_call(kernel, name='pair_sums', out_shape=jax.ShapeDtypeStruct((...]
    unnamed x2 -> x1, local copies, waits for them, and re-layouts: 0.65 us -> 1.32 us
    select_n x1 -> x0, other arithmetic: 0.55 us -> none  [local(): position = (right_order - lax.axis_index('band') * 2) % 4]
where the time goes in v2:
time: 36.8 us; the launch traced here: 36.6 us
  Pallas kernels  35.3 us (96%)
  local copies, waits for them, and re-layouts  1.32 us (4%)
    pallas_call x1, Pallas kernels, local(): pl.pallas_call(kernel, name='pair_sums', out_shape=jax.ShapeDtypeStruct((...  35.3 us
    unnamed x1, local copies, waits for them, and re-layouts  1.32 us

profile of v2, /device:TPU:1, one launch (start us, length us, event | category | flops | bytes accessed | tf_op | source)
XLA Modules:
  0.0 36.6 jit_solution(9089150461634993183)
XLA Ops:
  0.0 35.3 %pair_sums.1 = f32[32,128]{1,0:T(8,128)} custom-call(s32[4]{0:T(128)} %order_ref.1, f32[2,4,128,128]{3,2,1,0:T(8,128)} %bitcast.4, f32[2,2,128,128]{3,2,1,0:T(8,128)} %bitcast.5, s32[128,128]{1,0:T(8,128)} %bitcast.7, bf16[768,256]{1,0:T(8,128)(2,1)} %constant.6.clone.along_x_ref, bf16[256,768]{1,0:T(8,128)(2,1)} %constant.7.clone.along_y_ref, ...), custom_call_target="tpu_custom_call" | custom-call | tf_op jit(solution)/shard_map/pair_sums/pallas_call | solution.py:310
  35.3 1.3 %copy.9 = f32[2,4,4,128]{3,2,1,0:T(4,128)} copy(f32[2,4,4,128]{3,2,1,0:T(4,128)} %bitcast.6) | data formatting | bytes 32768

commit v3 on v2

--- a/solution.py
+++ b/solution.py
@@ -53,7 +53,7 @@
     order_ref, left_ref, right_ref, sphere_ref, along_x_ref, along_y_ref, trig_ref, out_ref,
     lefts, rights, own_right, sphere, along_x, along_y, trig,
     ky_t, val_t, kx_of, phase, acc, send, from_a, from_b, from_c, x_sum, tiles,
-    load_sem, pair_send, pair_recv, y_send, y_recv, x_send, x_recv, z_send, z_recv, known,
+    order, load_sem, pair_send, pair_recv, y_send, y_recv, x_send, x_recv, z_send, z_recv, known,
 ):
     g = lax.axis_index("grid")
     b = lax.axis_index("band")
@@ -72,6 +72,7 @@
         pltpu.make_async_copy(right_ref.at[:, c], rights.at[0, c], load_sem.at[4]),
         pltpu.make_async_copy(along_x_ref, along_x, load_sem.at[5]),
         pltpu.make_async_copy(along_y_ref, along_y, load_sem.at[6]),
+        pltpu.make_async_copy(order_ref, order, load_sem.at[7]),
     ]
     for load in loads:
         load.start()
@@ -79,28 +80,27 @@
     grid_up = up * SIDE + j
     grid_down = down * SIDE + j
     pair = g + 1 - 2 * c
+    h = lax.rem(lax.div(g, SIDE // 2), AH)
     z = lax.rem(lax.div(g, AC), AZ)
-    opposite = g + SIDE // 2 - SIDE * lax.rem(lax.div(g, SIDE // 2), AH)
-    along_z = [g + AC * (lax.rem(z + step, AZ) - z) for step in (1, 2, AZ - 1, AZ - 2)]
-    friends = along_z + [opposite, pair]
+    opposite = g + SIDE // 2 - SIDE * h
+    along_z = [g + AC * (lax.rem(z + step, AZ) - z) for step in (1, AZ - 1, 2, AZ - 2)]
+    near = [(along_z[0], b), (along_z[1], b), (pair, b), (g, 1 - b), (opposite, 1 - b)]
+    friends = [(grid, b) for grid in along_z + [opposite, pair]]
     barrier = pltpu.get_barrier_semaphore()
 
     def signal(sem, grid, band):
         pl.semaphore_signal(sem, inc=1, device_id=(grid, band), device_id_type=MESH)
 
-    signal(barrier, g - c, 1 - b)
-    signal(barrier, g - c + 1, 1 - b)
-    signal(barrier, grid_up, b)
-    signal(barrier, grid_down, b)
-    for friend in friends:
-        signal(barrier, friend, b)
+    meet = near + [(pair, 1 - b), (grid_up, b), (grid_down, b)]
+    for grid, band in meet:
+        signal(barrier, grid, band)
 
     def tell(step):
-        for friend in friends:
-            signal(known.at[step], friend, b)
+        for grid, band in near if step == 0 else friends:
+            signal(known.at[step], grid, band)
 
     def hear(step):
-        pl.semaphore_wait(known.at[step], len(friends))
+        pl.semaphore_wait(known.at[step], len(near if step == 0 else friends))
 
     def remote(source, target, sent, received, grid, band):
         return pltpu.make_async_remote_copy(
@@ -116,19 +116,6 @@
         remote(lefts.at[c], lefts.at[c], pair_send.at[0], pair_recv.at[0], pair, b),
         remote(own_right.at[:, 1 - c], rights.at[0, c], pair_send.at[1], pair_recv.at[1], pair, b),
     ]
-    loads[0].wait()
-    loads[1].wait()
-    pl.semaphore_wait(barrier, 4 + len(friends))
-
-    @pl.when(c == 0)
-    def _():
-        for copy in to_other:
-            copy.start()
-
-    for copy in to_pair:
-        copy.start()
-    tell(0)
-
     loads[2].wait()
     loads[3].wait()
     flipped = sphere[...].T
@@ -149,10 +136,12 @@
         phase[core, 0] = lanes(cosine, angle)
         phase[core, 1] = lanes(sine, angle)
 
-    @pl.when(c == 1)
-    def _():
-        for copy in to_other:
-            copy.start()
+    loads[0].wait()
+    loads[1].wait()
+    pl.semaphore_wait(barrier, len(meet))
+    for copy in to_other + to_pair:
+        copy.start()
+    tell(0)
 
     def transform(chunk, plane, combine):
         right_real = rights[chunk, plane, 0]
@@ -196,11 +185,9 @@
     def finish(chunk, channel, value):
         send[chunk, pl.ds(channel, NG, stride=8), :] = (acc[channel] + value).T
 
-    for load in loads[4:]:
+    for load in loads[4:7]:
         load.wait()
     transform(0, c, keep)
-    hear(0)
-    tell(1)
     for copy in to_pair:
         copy.wait_recv()
     transform(0, 1 - c, functools.partial(finish, 0))
@@ -241,14 +228,20 @@
         mine = pl.ds(pl.multiple_of(j * 8, 8), 8)
         tiles[chunk, mine] = x_sum[chunk, mine]
 
-        @pl.loop(1, SIDE)
-        def _(step):
-            to = lax.rem(j + step, SIDE)
-            theirs = pl.ds(pl.multiple_of(to * 8, 8), 8)
-            remote(
-                x_sum.at[chunk, theirs], tiles.at[chunk, mine],
-                z_send.at[chunk], z_recv.at[chunk], x * SIDE + to, b,
-            ).start()
+        for away_z in (4, 3, 5, 2, 6, 1, 7, 0):
+            for away in (2, 3, 0, 1):
+                if (away_z, away) == (0, 0):
+                    continue
+                to = (
+                    lax.rem(h + away // 2, AH) * AZ * AC
+                    + lax.rem(z + away_z, AZ) * AC
+                    + lax.rem(c + away % 2, AC)
+                )
+                theirs = pl.ds(pl.multiple_of(to * 8, 8), 8)
+                remote(
+                    x_sum.at[chunk, theirs], tiles.at[chunk, mine],
+                    z_send.at[chunk], z_recv.at[chunk], x * SIDE + to, b,
+                ).start()
 
     def z_wait(buffer, chunk, sem):
         many = buffer.at[chunk, pl.ds(0, (SIDE - 1) * 8)]
@@ -270,8 +263,12 @@
     native = x_copies(0)
     distant = x_copies(1)
     x_first(native)
-    hear(1)
-    tell(2)
+    hear(0)
+    tell(1)
+
+    @pl.when(c == 1)
+    def _():
+        x_second(0, native)
 
     def arrival(core):
         return remote(
@@ -280,18 +277,24 @@
 
     arrival(0).wait_recv()
     transform(1, 0, keep)
+    hear(1)
+    tell(2)
     arrival(1).wait_recv()
     transform(1, 1, functools.partial(finish, 1))
     x_first(distant)
-    x_second(0, native)
+    @pl.when(c == 0)
+    def _():
+        x_second(0, native)
+
     hear(2)
+    z_first(0, native)
     x_second(1, distant)
-    z_first(0, native)
     z_first(1, distant)
     values = z_last(0)
     values = values + z_last(1)
+    loads[7].wait()
     for column in range(4):
-        position = jnp.full((8, NG), lax.rem(order_ref[column] + 4 - 2 * b, 4), jnp.int32)
+        position = jnp.full((8, NG), lax.rem(order[column] + 4 - 2 * b, 4), jnp.int32)
         value = values[3]
         for at in range(3):
             value = jnp.where(position == at, values[at], value)
@@ -310,8 +313,8 @@
     result = pl.pallas_call(
         kernel,
         name="pair_sums",
-        out_shape=jax.ShapeDtypeStruct((32, NG), F32),
-        in_specs=[pl.BlockSpec(memory_space=pltpu.SMEM)] + [hbm] * 6,
+        out_shape=pltpu.VMEM((32, NG), F32),
+        in_specs=[hbm] * 7,
         out_specs=pl.BlockSpec(memory_space=pltpu.VMEM),
         scratch_shapes=[
             pltpu.VMEM((2, 2, 4, NG, NX), F32),
@@ -332,7 +335,8 @@
             pltpu.VMEM((2, 2, HALF, NG), F32),
             pltpu.VMEM((2, QUARTER, NG), F32),
             pltpu.VMEM((2, QUARTER, NG), F32),
-            dma((7,)), dma((2,)), dma((2,)), dma((2,)), dma((2,)),
+            pltpu.SMEM((4,), jnp.int32),
+            dma((8,)), dma((2,)), dma((2,)), dma((2,)), dma((2,)),
             dma((2, 6)), dma((2, 6)), dma((2,)), dma((2,)), pltpu.SemaphoreType.REGULAR((3,)),
         ],
         compiler_params=pltpu.CompilerParams(collective_id=0, has_side_effects=True),

time: 36.8 us -> 34.8 us (0.946)
  Pallas kernels: 35.3 us -> 34.1 us
  local copies, waits for them, and re-layouts: 1.32 us -> 0.61 us
    pallas_call x1, Pallas kernels: 35.3 us -> 34.1 us  [local(): pl.pallas_call(kernel, name='pair_sums', out_shape=pltpu.VMEM((32, NG), F...]
    unnamed x1, local copies, waits for them, and re-layouts: 1.32 us -> 0.61 us
where the time goes in v3:
time: 34.8 us; the launch traced here: 34.7 us
  Pallas kernels  34.1 us (98%)
  local copies, waits for them, and re-layouts  0.61 us (2%)
    pallas_call x1, Pallas kernels, local(): pl.pallas_call(kernel, name='pair_sums', out_shape=pltpu.VMEM((32, NG), F...  34.1 us

profile of v3, /device:TPU:1, one launch (start us, length us, event | category | flops | bytes accessed | tf_op | source)
XLA Modules:
  0.0 34.7 jit_solution(5804297101586990192)
XLA Ops:
  0.0 34.1 %pair_sums.1 = f32[32,128]{1,0:T(8,128)S(1)} custom-call(s32[4]{0:T(128)} %order_ref.1, f32[2,4,128,128]{3,2,1,0:T(8,128)} %bitcast.5, f32[2,2,128,128]{3,2,1,0:T(8,128)} %bitcast.6, s32[128,128]{1,0:T(8,128)} %bitcast.7, bf16[768,256]{1,0:T(8,128)(2,1)} %constant.6.clone.along_x_ref, bf16[256,768]{1,0:T(8,128)(2,1)} %constant.7.clone.along_y_ref, ...), custom_call_target="tpu_custom_call" | custom-call | tf_op jit(solution)/shard_map/pair_sums/pallas_call | solution.py:313
  34.1 0.6 %copy.9 = f32[2,4,4,128]{3,2,1,0:T(4,128)} copy(f32[2,4,4,128]{3,2,1,0:T(4,128)S(1)} %bitcast.4) | data formatting | bytes 32768

commit v4 on v3

--- a/solution.py
+++ b/solution.py
@@ -116,6 +116,15 @@
         remote(lefts.at[c], lefts.at[c], pair_send.at[0], pair_recv.at[0], pair, b),
         remote(own_right.at[:, 1 - c], rights.at[0, c], pair_send.at[1], pair_recv.at[1], pair, b),
     ]
+    loads[0].wait()
+    pl.semaphore_wait(barrier, len(meet))
+    for copy in to_other:
+        copy.start()
+    loads[1].wait()
+    for copy in to_pair:
+        copy.start()
+    tell(0)
+
     loads[2].wait()
     loads[3].wait()
     flipped = sphere[...].T
@@ -135,13 +144,6 @@
         angle = (kz * (g - c + core)) & 127
         phase[core, 0] = lanes(cosine, angle)
         phase[core, 1] = lanes(sine, angle)
-
-    loads[0].wait()
-    loads[1].wait()
-    pl.semaphore_wait(barrier, len(meet))
-    for copy in to_other + to_pair:
-        copy.start()
-    tell(0)
 
     def transform(chunk, plane, combine):
         right_real = rights[chunk, plane, 0]
@@ -280,12 +282,13 @@
     hear(1)
     tell(2)
     arrival(1).wait_recv()
-    transform(1, 1, functools.partial(finish, 1))
-    x_first(distant)
+
     @pl.when(c == 0)
     def _():
         x_second(0, native)
 
+    transform(1, 1, functools.partial(finish, 1))
+    x_first(distant)
     hear(2)
     z_first(0, native)
     x_second(1, distant)

time: 34.8 us -> 33.6 us (0.966)
  Pallas kernels: 34.1 us -> 32.9 us
    pallas_call x1, Pallas kernels: 34.1 us -> 32.9 us  [local(): pl.pallas_call(kernel, name='pair_sums', out_shape=pltpu.VMEM((32, NG), F...]
where the time goes in v4:
time: 33.6 us; the launch traced here: 33.5 us
  Pallas kernels  32.9 us (98%)
  local copies, waits for them, and re-layouts  0.61 us (2%)
    pallas_call x1, Pallas kernels, local(): pl.pallas_call(kernel, name='pair_sums', out_shape=pltpu.VMEM((32, NG), F...  32.9 us

profile of v4, /device:TPU:1, one launch (start us, length us, event | category | flops | bytes accessed | tf_op | source)
XLA Modules:
  0.0 33.5 jit_solution(9044333241366524020)
XLA Ops:
  0.0 32.9 %pair_sums.1 = f32[32,128]{1,0:T(8,128)S(1)} custom-call(s32[4]{0:T(128)} %order_ref.1, f32[2,4,128,128]{3,2,1,0:T(8,128)} %bitcast.5, f32[2,2,128,128]{3,2,1,0:T(8,128)} %bitcast.6, s32[128,128]{1,0:T(8,128)} %bitcast.7, bf16[768,256]{1,0:T(8,128)(2,1)} %constant.6.clone.along_x_ref, bf16[256,768]{1,0:T(8,128)(2,1)} %constant.7.clone.along_y_ref, ...), custom_call_target="tpu_custom_call" | custom-call | tf_op jit(solution)/shard_map/pair_sums/pallas_call | solution.py:316
  32.9 0.6 %copy.9 = f32[2,4,4,128]{3,2,1,0:T(4,128)} copy(f32[2,4,4,128]{3,2,1,0:T(4,128)S(1)} %bitcast.4) | data formatting | bytes 32768

commit v5 on v4

--- a/solution.py
+++ b/solution.py
@@ -145,54 +145,81 @@
         phase[core, 0] = lanes(cosine, angle)
         phase[core, 1] = lanes(sine, angle)
 
-    def transform(chunk, plane, combine):
+    def along_rows(chunk, plane, half):
         right_real = rights[chunk, plane, 0]
         right_imag = rights[chunk, plane, 1]
-        index = kx_of[...]
-        for half in range(2):
-            columns = []
-            for n in (2 * half, 2 * half + 1):
-                left_real = lefts[plane, 0, n]
-                left_imag = lefts[plane, 1, n]
-                field = jnp.concatenate(
-                    [
-                        left_real * right_real + left_imag * right_imag,
-                        left_real * right_imag - left_imag * right_real,
-                    ],
-                    axis=1,
-                )
-                high, low = split(field)
-                moved = jnp.dot(
-                    jnp.concatenate([high, low, high], axis=1),
-                    along_x[...],
-                    preferred_element_type=F32,
-                )
-                columns.append(jnp.concatenate([moved[:, :NX], moved[:, NX:]], axis=0))
-            high, low = split(jnp.concatenate(columns, axis=1))
-            plane_waves = jnp.dot(
-                along_y[...],
-                jnp.concatenate([high, high, low], axis=0),
+        columns = []
+        for n in (2 * half, 2 * half + 1):
+            left_real = lefts[plane, 0, n]
+            left_imag = lefts[plane, 1, n]
+            field = jnp.concatenate(
+                [
+                    left_real * right_real + left_imag * right_imag,
+                    left_real * right_imag - left_imag * right_real,
+                ],
+                axis=1,
+            )
+            high, low = split(field)
+            moved = jnp.dot(
+                jnp.concatenate([high, low, high], axis=1),
+                along_x[...],
                 preferred_element_type=F32,
             )
-            for at, n in enumerate((2 * half, 2 * half + 1)):
-                real = lanes(plane_waves[:NG, at * NX : (at + 1) * NX], index)
-                imag = lanes(plane_waves[NG:, at * NX : (at + 1) * NX], index)
-                cosines, sines = phase[plane, 0], phase[plane, 1]
-                combine(n, real * cosines + imag * sines)
-                combine(n + 4, imag * cosines - real * sines)
-
-    def keep(channel, value):
-        acc[channel] = value
-
-    def finish(chunk, channel, value):
-        send[chunk, pl.ds(channel, NG, stride=8), :] = (acc[channel] + value).T
+            columns.append(jnp.concatenate([moved[:, :NX], moved[:, NX:]], axis=0))
+        return split(jnp.concatenate(columns, axis=1))
+
+    def along_columns(rows):
+        high, low = rows
+        return jnp.dot(
+            along_y[...], jnp.concatenate([high, high, low], axis=0), preferred_element_type=F32
+        )
+
+    def pick(plane, waves, half):
+        index = kx_of[...]
+        cosines, sines = phase[plane, 0], phase[plane, 1]
+        picked = {}
+        for at in range(2):
+            real = lanes(waves[:NG, at * NX : (at + 1) * NX], index)
+            imag = lanes(waves[NG:, at * NX : (at + 1) * NX], index)
+            n = 2 * half + at
+            picked[n] = real * cosines + imag * sines
+            picked[n + 4] = imag * cosines - real * sines
+        return picked
+
+    def ship(chunk, channel, value):
+        send[chunk, pl.ds(channel, NG, stride=8), :] = value.T
+
+    def native_first(plane):
+        for half in range(2):
+            picked = pick(plane, along_columns(along_rows(0, plane, half)), half)
+            for channel, value in picked.items():
+                acc[channel] = value
+
+    def native_second(plane):
+        for half in range(2):
+            picked = pick(plane, along_columns(along_rows(0, plane, half)), half)
+            for channel, value in picked.items():
+                ship(0, channel, acc[channel] + value)
+
+    def distant_both():
+        def total(half, waves):
+            first, second = (pick(plane, waves[plane], half) for plane in range(2))
+            for channel in first:
+                ship(1, channel, first[channel] + second[channel])
+
+        rows = [along_rows(1, plane, 0) for plane in range(2)]
+        waves = [along_columns(value) for value in rows]
+        rows = [along_rows(1, plane, 1) for plane in range(2)]
+        total(0, waves)
+        waves = [along_columns(value) for value in rows]
+        total(1, waves)
 
     for load in loads[4:7]:
         load.wait()
-    transform(0, c, keep)
+    native_first(c)
     for copy in to_pair:
         copy.wait_recv()
-    transform(0, 1 - c, functools.partial(finish, 0))
+    native_second(1 - c)
 
     def part(chunk, quarter, half):
         start = pl.multiple_of(quarter * QUARTER + half * HALF, HALF)
@@ -210,7 +237,11 @@
         ]
 
     def x_first(copies):
-        for copy in copies[:4]:
+        for copy in copies[:2]:
+            copy.start()
+
+    def x_direct(copies):
+        for copy in copies[2:4]:
             copy.start()
 
     def x_second(chunk, copies):
@@ -265,6 +296,7 @@
     native = x_copies(0)
     distant = x_copies(1)
     x_first(native)
+    x_direct(native)
     hear(0)
     tell(1)
 
@@ -278,20 +310,29 @@
         )
 
     arrival(0).wait_recv()
-    transform(1, 0, keep)
+    arrival(1).wait_recv()
+    distant_both()
+    x_first(distant)
     hear(1)
     tell(2)
-    arrival(1).wait_recv()
 
     @pl.when(c == 0)
     def _():
         x_second(0, native)
-
-    transform(1, 1, functools.partial(finish, 1))
-    x_first(distant)
+        x_direct(distant)
+        x_second(1, distant)
+
+    @pl.when(c == 1)
+    def _():
+        x_direct(distant)
+
     hear(2)
     z_first(0, native)
-    x_second(1, distant)
+
+    @pl.when(c == 1)
+    def _():
+        x_second(1, distant)
+
     z_first(1, distant)
     values = z_last(0)
     values = values + z_last(1)

time: 33.6 us -> 31.5 us (0.938)
  Pallas kernels: 32.9 us -> 30.8 us
    pallas_call x1, Pallas kernels: 32.9 us -> 30.8 us  [local(): pl.pallas_call(kernel, name='pair_sums', out_shape=pltpu.VMEM((32, NG), F...]
where the time goes in v5:
time: 31.5 us
  Pallas kernels  30.8 us (98%)
  local copies, waits for them, and re-layouts  0.61 us (2%)
    pallas_call x1, Pallas kernels, local(): pl.pallas_call(kernel, name='pair_sums', out_shape=pltpu.VMEM((32, NG), F...  30.8 us

profile of v5, /device:TPU:1, one launch (start us, length us, event | category | flops | bytes accessed | tf_op | source)
XLA Modules:
  0.0 31.5 jit_solution(17292466268902635025)
XLA Ops:
  0.0 30.8 %pair_sums.1 = f32[32,128]{1,0:T(8,128)S(1)} custom-call(s32[4]{0:T(128)} %order_ref.1, f32[2,4,128,128]{3,2,1,0:T(8,128)} %bitcast.5, f32[2,2,128,128]{3,2,1,0:T(8,128)} %bitcast.6, s32[128,128]{1,0:T(8,128)} %bitcast.7, bf16[768,256]{1,0:T(8,128)(2,1)} %constant.6.clone.along_x_ref, bf16[256,768]{1,0:T(8,128)(2,1)} %constant.7.clone.along_y_ref, ...), custom_call_target="tpu_custom_call" | custom-call | tf_op jit(solution)/shard_map/pair_sums/pallas_call | solution.py:357
  30.8 0.6 %copy.9 = f32[2,4,4,128]{3,2,1,0:T(4,128)} copy(f32[2,4,4,128]{3,2,1,0:T(4,128)S(1)} %bitcast.4) | data formatting | bytes 32768

commit v6 on v5

--- a/solution.py
+++ b/solution.py
@@ -16,6 +16,8 @@
 SIDE = AH * AZ * AC
 QUARTER = SIDE * 8
 HALF = QUARTER // 2
+PIECE = HALF // 2
+PLACE = (0, 2, 1, 3)
 MESH = pl.DeviceIdType.MESH
 F32 = jnp.float32
 BF16 = jnp.bfloat16
@@ -67,12 +69,17 @@
     loads = [
         pltpu.make_async_copy(right_ref, own_right, load_sem.at[0]),
         pltpu.make_async_copy(left_ref, lefts.at[c], load_sem.at[1]),
-        pltpu.make_async_copy(sphere_ref, sphere, load_sem.at[2]),
-        pltpu.make_async_copy(trig_ref, trig, load_sem.at[3]),
-        pltpu.make_async_copy(right_ref.at[:, c], rights.at[0, c], load_sem.at[4]),
-        pltpu.make_async_copy(along_x_ref, along_x, load_sem.at[5]),
-        pltpu.make_async_copy(along_y_ref, along_y, load_sem.at[6]),
-        pltpu.make_async_copy(order_ref, order, load_sem.at[7]),
+        pltpu.make_async_copy(trig_ref, trig, load_sem.at[2]),
+        pltpu.make_async_copy(right_ref.at[:, c], rights.at[0, c], load_sem.at[3]),
+        pltpu.make_async_copy(along_x_ref, along_x, load_sem.at[4]),
+        pltpu.make_async_copy(along_y_ref, along_y, load_sem.at[5]),
+        pltpu.make_async_copy(order_ref, order, load_sem.at[6]),
+    ]
+    loads += [
+        pltpu.make_async_copy(
+            sphere_ref.at[:, at], sphere.at[:, PLACE[at]], load_sem.at[8 + at]
+        )
+        for at in range(4)
     ]
     for load in loads:
         load.start()
@@ -82,6 +89,7 @@
     pair = g + 1 - 2 * c
     h = lax.rem(lax.div(g, SIDE // 2), AH)
     z = lax.rem(lax.div(g, AC), AZ)
+    q = lax.div(z, 4) * 16 + h * 8 + lax.rem(z, 4) * AC + c
     opposite = g + SIDE // 2 - SIDE * h
     along_z = [g + AC * (lax.rem(z + step, AZ) - z) for step in (1, AZ - 1, 2, AZ - 2)]
     near = [(along_z[0], b), (along_z[1], b), (pair, b), (g, 1 - b), (opposite, 1 - b)]
@@ -125,9 +133,10 @@
         copy.start()
     tell(0)
 
+    for load in loads[7:]:
+        load.wait()
     loads[2].wait()
-    loads[3].wait()
-    flipped = sphere[...].T
+    flipped = sphere[...].reshape(NG, NG).T
     ky_t[...] = (flipped >> 7) & 127
     val_t[...] = ((flipped >> 14) << 7) | (flipped & 127)
     rows = lax.broadcasted_iota(jnp.int32, (NG, NG), 0)
@@ -214,73 +223,87 @@
         waves = [along_columns(value) for value in rows]
         total(1, waves)
 
-    for load in loads[4:7]:
+    for load in loads[3:6]:
         load.wait()
     native_first(c)
+    hear(0)
+    tell(1)
     for copy in to_pair:
         copy.wait_recv()
     native_second(1 - c)
 
-    def part(chunk, quarter, half):
-        start = pl.multiple_of(quarter * QUARTER + half * HALF, HALF)
-        return send.at[chunk, pl.ds(start, HALF)]
-
-    def x_copies(chunk):
-        sent, received = x_send.at[chunk], x_recv.at[chunk]
-        return [
-            remote(part(chunk, across, 0), from_a.at[chunk, 0], sent.at[0], received.at[0], grid_up, b),
-            remote(part(chunk, across, 1), from_a.at[chunk, 1], sent.at[1], received.at[1], grid_down, b),
-            remote(part(chunk, up, 1), from_b.at[chunk, 0], sent.at[2], received.at[2], grid_up, b),
-            remote(part(chunk, down, 0), from_b.at[chunk, 1], sent.at[3], received.at[3], grid_down, b),
-            remote(part(chunk, up, 0), from_c.at[chunk, 0], sent.at[4], received.at[4], grid_up, b),
-            remote(part(chunk, down, 1), from_c.at[chunk, 1], sent.at[5], received.at[5], grid_down, b),
-        ]
-
-    def x_first(copies):
-        for copy in copies[:2]:
-            copy.start()
-
-    def x_direct(copies):
-        for copy in copies[2:4]:
-            copy.start()
-
-    def x_second(chunk, copies):
-        for way, quarter in enumerate((up, down)):
-            copies[way].wait_recv()
-            ref = part(chunk, quarter, way)
-            ref[...] = ref[...] + from_a[chunk, way]
-            copies[4 + way].start()
-
-    def z_first(chunk, copies):
-        for copy in copies[2:]:
-            copy.wait_recv()
-        for half in range(2):
-            x_sum[chunk, pl.ds(half * HALF, HALF)] = (
-                part(chunk, x, half)[...] + from_c[chunk, half] + from_b[chunk, 1 - half]
+    def part(chunk, quarter, late, way):
+        start = pl.multiple_of(quarter * QUARTER + late * HALF + way * PIECE, PIECE)
+        return send.at[chunk, pl.ds(start, PIECE)]
+
+    class Hop:
+        def __init__(self, chunk, late):
+            self.at = chunk, late
+            sent, received = x_send.at[chunk, late], x_recv.at[chunk, late]
+            self.buffers = [ref.at[chunk, late] for ref in (from_a, from_b, from_c)]
+            routes = (
+                (across, 0, 0, grid_up), (across, 1, 0, grid_down),
+                (up, 1, 1, grid_up), (down, 0, 1, grid_down),
+                (up, 0, 2, grid_up), (down, 1, 2, grid_down),
             )
-        mine = pl.ds(pl.multiple_of(j * 8, 8), 8)
-        tiles[chunk, mine] = x_sum[chunk, mine]
-
-        for away_z in (4, 3, 5, 2, 6, 1, 7, 0):
-            for away in (2, 3, 0, 1):
-                if (away_z, away) == (0, 0):
-                    continue
-                to = (
-                    lax.rem(h + away // 2, AH) * AZ * AC
-                    + lax.rem(z + away_z, AZ) * AC
-                    + lax.rem(c + away % 2, AC)
+            self.copies = [
+                remote(
+                    part(chunk, quarter, late, way), self.buffers[kind].at[number % 2],
+                    sent.at[number], received.at[number], to, b,
                 )
-                theirs = pl.ds(pl.multiple_of(to * 8, 8), 8)
-                remote(
-                    x_sum.at[chunk, theirs], tiles.at[chunk, mine],
-                    z_send.at[chunk], z_recv.at[chunk], x * SIDE + to, b,
-                ).start()
+                for number, (quarter, way, kind, to) in enumerate(routes)
+            ]
+
+        def first(self):
+            for copy in self.copies[:2]:
+                copy.start()
+
+        def direct(self):
+            for copy in self.copies[2:4]:
+                copy.start()
+
+        def second(self):
+            for way, quarter in enumerate((up, down)):
+                self.copies[way].wait_recv()
+                ref = part(self.at[0], quarter, self.at[1], way)
+                ref[...] = ref[...] + self.buffers[0][way]
+                self.copies[4 + way].start()
+
+        def spread(self):
+            chunk, late = self.at
+            for copy in self.copies[2:]:
+                copy.wait_recv()
+            for way in range(2):
+                x_sum[chunk, pl.ds(late * HALF + way * PIECE, PIECE)] = (
+                    part(chunk, x, late, way)[...]
+                    + self.buffers[2][way]
+                    + self.buffers[1][1 - way]
+                )
+            mine = pl.ds(pl.multiple_of(q * 8, 8), 8)
+            for owner_z in ((0, 1, 2, 3), (4, 7, 5, 6))[late]:
+                for owner_h in range(2):
+                    for owner_c in (1, 0):
+                        to = late * 16 + owner_h * 8 + owner_z % 4 * 2 + owner_c
+                        theirs = pl.ds(to * 8, 8)
+                        owner = x * SIDE + (owner_h * AZ + owner_z) * AC + owner_c
+
+                        @pl.when(q != to)
+                        def _(theirs=theirs, owner=owner):
+                            remote(
+                                x_sum.at[chunk, theirs], tiles.at[chunk, mine],
+                                z_send.at[chunk], z_recv.at[chunk], owner, b,
+                            ).start()
+
+            @pl.when(lax.div(z, 4) == late)
+            def _():
+                tiles[chunk, mine] = x_sum[chunk, mine]
 
     def z_wait(buffer, chunk, sem):
         many = buffer.at[chunk, pl.ds(0, (SIDE - 1) * 8)]
         pltpu.make_async_copy(many, many, sem.at[chunk]).wait()
 
-    index = jnp.broadcast_to((sphere[pl.ds(g, 1), :] >> 7) & 127, (8, NG))
+    own = sphere[x, lax.div(z, 4) * 2 + h, pl.ds(lax.rem(z, 4) * AC + c, 1), :]
+    index = jnp.broadcast_to((own >> 7) & 127, (8, NG))
     factor = 1.0 / (NG * NG * NX) ** 0.5
 
     def z_last(chunk):
@@ -293,16 +316,20 @@
             values.append(lanes(total, index) * factor)
         return values
 
-    native = x_copies(0)
-    distant = x_copies(1)
-    x_first(native)
-    x_direct(native)
-    hear(0)
-    tell(1)
+    (native, native_late), (distant, distant_late) = (
+        [Hop(chunk, late) for late in range(2)] for chunk in range(2)
+    )
+    native.first()
+    native_late.first()
+    native.direct()
+    native_late.direct()
 
     @pl.when(c == 1)
     def _():
-        x_second(0, native)
+        native.second()
+        native_late.second()
+        hear(1)
+        tell(2)
 
     def arrival(core):
         return remote(
@@ -311,32 +338,33 @@
 
     arrival(0).wait_recv()
     arrival(1).wait_recv()
-    distant_both()
-    x_first(distant)
-    hear(1)
-    tell(2)
 
     @pl.when(c == 0)
     def _():
-        x_second(0, native)
-        x_direct(distant)
-        x_second(1, distant)
-
-    @pl.when(c == 1)
+        hear(1)
+        tell(2)
+
+    distant_both()
+    distant.first()
+
+    @pl.when(c == 0)
     def _():
-        x_direct(distant)
-
+        native.second()
+        native_late.second()
+
+    distant.direct()
+    distant_late.first()
+    distant.second()
+    distant_late.direct()
     hear(2)
-    z_first(0, native)
-
-    @pl.when(c == 1)
-    def _():
-        x_second(1, distant)
-
-    z_first(1, distant)
+    native.spread()
+    distant_late.second()
+    native_late.spread()
+    distant.spread()
+    distant_late.spread()
     values = z_last(0)
     values = values + z_last(1)
-    loads[7].wait()
+    loads[6].wait()
     for column in range(4):
         position = jnp.full((8, NG), lax.rem(order[column] + 4 - 2 * b, 4), jnp.int32)
         value = values[3]
@@ -344,8 +372,11 @@
             value = jnp.where(position == at, values[at], value)
         out_ref[pl.ds(column, 8, stride=4), :] = value
 
-    for copy in to_pair + to_other + native + distant:
+    for copy in to_pair + to_other:
         copy.wait_send()
+    for hop in (native, native_late, distant, distant_late):
+        for copy in hop.copies:
+            copy.wait_send()
     for chunk in range(2):
         z_wait(x_sum, chunk, z_send)
 
@@ -364,7 +395,7 @@
             pltpu.VMEM((2, 2, 4, NG, NX), F32),
             pltpu.VMEM((2, 2, 2, NG, NX), F32),
             pltpu.VMEM((2, 2, NG, NX), F32),
-            pltpu.VMEM((NG, NG), jnp.int32),
+            pltpu.VMEM((4, 4, 8, NG), jnp.int32),
             pltpu.VMEM((6 * NG, 2 * NG), BF16),
             pltpu.VMEM((2 * NG, 6 * NG), BF16),
             pltpu.VMEM((8, NG), F32),
@@ -374,21 +405,21 @@
             pltpu.VMEM((2, 2, NG, NG), F32),
             pltpu.VMEM((8, NG, NG), F32),
             pltpu.VMEM((2, AX * QUARTER, NG), F32),
-            pltpu.VMEM((2, 2, HALF, NG), F32),
-            pltpu.VMEM((2, 2, HALF, NG), F32),
-            pltpu.VMEM((2, 2, HALF, NG), F32),
+            pltpu.VMEM((2, 2, 2, PIECE, NG), F32),
+            pltpu.VMEM((2, 2, 2, PIECE, NG), F32),
+            pltpu.VMEM((2, 2, 2, PIECE, NG), F32),
             pltpu.VMEM((2, QUARTER, NG), F32),
             pltpu.VMEM((2, QUARTER, NG), F32),
             pltpu.SMEM((4,), jnp.int32),
-            dma((8,)), dma((2,)), dma((2,)), dma((2,)), dma((2,)),
-            dma((2, 6)), dma((2, 6)), dma((2,)), dma((2,)), pltpu.SemaphoreType.REGULAR((3,)),
+            dma((12,)), dma((2,)), dma((2,)), dma((2,)), dma((2,)),
+            dma((2, 2, 6)), dma((2, 2, 6)), dma((2,)), dma((2,)), pltpu.SemaphoreType.REGULAR((3,)),
         ],
         compiler_params=pltpu.CompilerParams(collective_id=0, has_side_effects=True),
     )(
         right_order,
         left_bands.reshape(2, 4, NG, NX),
         right_bands.reshape(2, 2, NG, NX),
-        sphere_index.reshape(NG, NG),
+        sphere_index.reshape(4, 4, 8, NG),
         jnp.asarray(along_x),
         jnp.asarray(along_y),
         jnp.asarray(trig),

time: 31.5 us -> 30.7 us (0.975)
  Pallas kernels: 30.8 us -> 30 us
    pallas_call x1, Pallas kernels: 30.8 us -> 30 us  [local(): pl.pallas_call(kernel, name='pair_sums', out_shape=pltpu.VMEM((32, NG), F...]
where the time goes in v6:
time: 30.7 us
  Pallas kernels  30 us (98%)
  local copies, waits for them, and re-layouts  0.61 us (2%)
    pallas_call x1, Pallas kernels, local(): pl.pallas_call(kernel, name='pair_sums', out_shape=pltpu.VMEM((32, NG), F...  30 us

profile of v6, /device:TPU:1, one launch (start us, length us, event | category | flops | bytes accessed | tf_op | source)
XLA Modules:
  0.0 30.7 jit_solution(11686455685310228190)
XLA Ops:
  0.0 30.0 %pair_sums.1 = f32[32,128]{1,0:T(8,128)S(1)} custom-call(s32[4]{0:T(128)} %order_ref.1, f32[2,4,128,128]{3,2,1,0:T(8,128)} %bitcast.5, f32[2,2,128,128]{3,2,1,0:T(8,128)} %bitcast.6, s32[4,4,8,128]{3,2,1,0:T(8,128)} %bitcast.7, bf16[768,256]{1,0:T(8,128)(2,1)} %constant.6.clone.along_x_ref, bf16[256,768]{1,0:T(8,128)(2,1)} %constant.7.clone.along_y_ref, ...), custom_call_target="tpu_custom_call" | custom-call | tf_op jit(solution)/shard_map/pair_sums/pallas_call | solution.py:388
  30.0 0.6 %copy.9 = f32[2,4,4,128]{3,2,1,0:T(4,128)} copy(f32[2,4,4,128]{3,2,1,0:T(4,128)S(1)} %bitcast.4) | data formatting | bytes 32768

commit v7 on v6

--- a/solution.py
+++ b/solution.py
@@ -91,24 +91,30 @@
     z = lax.rem(lax.div(g, AC), AZ)
     q = lax.div(z, 4) * 16 + h * 8 + lax.rem(z, 4) * AC + c
     opposite = g + SIDE // 2 - SIDE * h
-    along_z = [g + AC * (lax.rem(z + step, AZ) - z) for step in (1, AZ - 1, 2, AZ - 2)]
-    near = [(along_z[0], b), (along_z[1], b), (pair, b), (g, 1 - b), (opposite, 1 - b)]
-    friends = [(grid, b) for grid in along_z + [opposite, pair]]
+    along_z = [(g + AC * (lax.rem(z + step, AZ) - z), b) for step in (1, AZ - 1, 2, AZ - 2)]
+    close = [(pair, b), (g, 1 - b), (pair, 1 - b)]
+    near = along_z[:2] + [(grid_up, b), (grid_down, b), (opposite, 1 - b)]
     barrier = pltpu.get_barrier_semaphore()
 
-    def signal(sem, grid, band):
-        pl.semaphore_signal(sem, inc=1, device_id=(grid, band), device_id_type=MESH)
-
-    meet = near + [(pair, 1 - b), (grid_up, b), (grid_down, b)]
-    for grid, band in meet:
-        signal(barrier, grid, band)
+    def signal(sem, devices):
+        for grid, band in devices:
+            pl.semaphore_signal(sem, inc=1, device_id=(grid, band), device_id_type=MESH)
+
+    signal(barrier, close)
+
+    @pl.when(c == 1)
+    def _():
+        signal(barrier, near)
 
     def tell(step):
-        for grid, band in near if step == 0 else friends:
-            signal(known.at[step], grid, band)
+        others = near + [(g, 1 - b)] if step == 0 else along_z + [(opposite, b)]
+
+        @pl.when(c == 1)
+        def _():
+            signal(known.at[step], [(pair, b)] + others)
 
     def hear(step):
-        pl.semaphore_wait(known.at[step], len(near if step == 0 else friends))
+        pl.semaphore_wait(known.at[step], jnp.where(c == 1, 6 if step == 0 else 5, 1))
 
     def remote(source, target, sent, received, grid, band):
         return pltpu.make_async_remote_copy(
@@ -125,7 +131,7 @@
         remote(own_right.at[:, 1 - c], rights.at[0, c], pair_send.at[1], pair_recv.at[1], pair, b),
     ]
     loads[0].wait()
-    pl.semaphore_wait(barrier, len(meet))
+    pl.semaphore_wait(barrier, jnp.where(c == 1, len(close) + len(near), len(close)))
     for copy in to_other:
         copy.start()
     loads[1].wait()
@@ -319,6 +325,11 @@
     (native, native_late), (distant, distant_late) = (
         [Hop(chunk, late) for late in range(2)] for chunk in range(2)
     )
+
+    @pl.when(c == 0)
+    def _():
+        hear(1)
+
     native.first()
     native_late.first()
     native.direct()
@@ -326,10 +337,10 @@
 
     @pl.when(c == 1)
     def _():
+        hear(1)
+        tell(2)
         native.second()
         native_late.second()
-        hear(1)
-        tell(2)
 
     def arrival(core):
         return remote(
@@ -338,11 +349,10 @@
 
     arrival(0).wait_recv()
     arrival(1).wait_recv()
-
-    @pl.when(c == 0)
-    def _():
-        hear(1)
-        tell(2)
+    @pl.when(c == 1)
+    def _():
+        hear(2)
+        tell(3)
 
     distant_both()
     distant.first()
@@ -351,16 +361,26 @@
     def _():
         native.second()
         native_late.second()
-
-    distant.direct()
-    distant_late.first()
-    distant.second()
+        distant_late.first()
+        distant.direct()
+        hear(2)
+        distant.second()
+        hear(3)
+        native.spread()
+        native_late.spread()
+
+    @pl.when(c == 1)
+    def _():
+        hear(3)
+        native.spread()
+        distant_late.first()
+        distant.direct()
+        native_late.spread()
+        distant.second()
+
+    distant.spread()
     distant_late.direct()
-    hear(2)
-    native.spread()
     distant_late.second()
-    native_late.spread()
-    distant.spread()
     distant_late.spread()
     values = z_last(0)
     values = values + z_last(1)
@@ -412,7 +432,7 @@
             pltpu.VMEM((2, QUARTER, NG), F32),
             pltpu.SMEM((4,), jnp.int32),
             dma((12,)), dma((2,)), dma((2,)), dma((2,)), dma((2,)),
-            dma((2, 2, 6)), dma((2, 2, 6)), dma((2,)), dma((2,)), pltpu.SemaphoreType.REGULAR((3,)),
+            dma((2, 2, 6)), dma((2, 2, 6)), dma((2,)), dma((2,)), pltpu.SemaphoreType.REGULAR((4,)),
         ],
         compiler_params=pltpu.CompilerParams(collective_id=0, has_side_effects=True),
     )(

time: 30.7 us -> 30.4 us (level)
    pallas_call x1, Pallas kernels: 30 us -> 29.7 us  [local(): pl.pallas_call(kernel, name='pair_sums', out_shape=pltpu.VMEM((32, NG), F...]
where the time goes in v7:
time: 30.4 us; the launch traced here: 30.3 us
  Pallas kernels  29.7 us (98%)
  local copies, waits for them, and re-layouts  0.61 us (2%)
    pallas_call x1, Pallas kernels, local(): pl.pallas_call(kernel, name='pair_sums', out_shape=pltpu.VMEM((32, NG), F...  29.7 us

profile of v7, /device:TPU:1, one launch (start us, length us, event | category | flops | bytes accessed | tf_op | source)
XLA Modules:
  0.0 30.3 jit_solution(8621322445540940717)
XLA Ops:
  0.0 29.7 %pair_sums.1 = f32[32,128]{1,0:T(8,128)S(1)} custom-call(s32[4]{0:T(128)} %order_ref.1, f32[2,4,128,128]{3,2,1,0:T(8,128)} %bitcast.5, f32[2,2,128,128]{3,2,1,0:T(8,128)} %bitcast.6, s32[4,4,8,128]{3,2,1,0:T(8,128)} %bitcast.7, bf16[768,256]{1,0:T(8,128)(2,1)} %constant.6.clone.along_x_ref, bf16[256,768]{1,0:T(8,128)(2,1)} %constant.7.clone.along_y_ref, ...), custom_call_target="tpu_custom_call" | custom-call | tf_op jit(solution)/shard_map/pair_sums/pallas_call | solution.py:408
  29.7 0.6 %copy.9 = f32[2,4,4,128]{3,2,1,0:T(4,128)} copy(f32[2,4,4,128]{3,2,1,0:T(4,128)S(1)} %bitcast.4) | data formatting | bytes 32768

commit v8 on v7

--- a/solution.py
+++ b/solution.py
@@ -54,7 +54,7 @@
 def kernel(
     order_ref, left_ref, right_ref, sphere_ref, along_x_ref, along_y_ref, trig_ref, out_ref,
     lefts, rights, own_right, sphere, along_x, along_y, trig,
-    ky_t, val_t, kx_of, phase, acc, send, from_a, from_b, from_c, x_sum, tiles,
+    ky_t, val_t, kx_of, phase, acc, send, from_a, from_b, from_c, from_all, x_sum, tiles,
     order, load_sem, pair_send, pair_recv, y_send, y_recv, x_send, x_recv, z_send, z_recv, known,
 ):
     g = lax.axis_index("grid")
@@ -107,14 +107,14 @@
         signal(barrier, near)
 
     def tell(step):
-        others = near + [(g, 1 - b)] if step == 0 else along_z + [(opposite, b)]
+        others = near + [(g, 1 - b)] if step == 0 else along_z + near[2:4] + [(opposite, b)]
 
         @pl.when(c == 1)
         def _():
             signal(known.at[step], [(pair, b)] + others)
 
     def hear(step):
-        pl.semaphore_wait(known.at[step], jnp.where(c == 1, 6 if step == 0 else 5, 1))
+        pl.semaphore_wait(known.at[step], jnp.where(c == 1, 6 if step == 0 else 7, 1))
 
     def remote(source, target, sent, received, grid, band):
         return pltpu.make_async_remote_copy(
@@ -242,11 +242,35 @@
         start = pl.multiple_of(quarter * QUARTER + late * HALF + way * PIECE, PIECE)
         return send.at[chunk, pl.ds(start, PIECE)]
 
-    class Hop:
-        def __init__(self, chunk, late):
-            self.at = chunk, late
-            sent, received = x_send.at[chunk, late], x_recv.at[chunk, late]
-            self.buffers = [ref.at[chunk, late] for ref in (from_a, from_b, from_c)]
+    def whole(quarter, late):
+        start = pl.multiple_of(quarter * QUARTER + late * HALF, HALF)
+        return send.at[1, pl.ds(start, HALF)]
+
+    def send_tiles(chunk, late):
+        mine = pl.ds(pl.multiple_of(q * 8, 8), 8)
+        for owner_z in ((0, 1, 2, 3), (4, 7, 5, 6))[late]:
+            for owner_h in range(2):
+                for owner_c in (1, 0):
+                    to = late * 16 + owner_h * 8 + owner_z % 4 * 2 + owner_c
+                    theirs = pl.ds(to * 8, 8)
+                    owner = x * SIDE + (owner_h * AZ + owner_z) * AC + owner_c
+
+                    @pl.when(q != to)
+                    def _(theirs=theirs, owner=owner):
+                        remote(
+                            x_sum.at[chunk, theirs], tiles.at[chunk, mine],
+                            z_send.at[chunk], z_recv.at[chunk], owner, b,
+                        ).start()
+
+        @pl.when(lax.div(z, 4) == late)
+        def _():
+            tiles[chunk, mine] = x_sum[chunk, mine]
+
+    class Relay:
+        def __init__(self, late):
+            self.late = late
+            sent, received = x_send.at[0, late], x_recv.at[0, late]
+            self.buffers = [ref.at[late] for ref in (from_a, from_b, from_c)]
             routes = (
                 (across, 0, 0, grid_up), (across, 1, 0, grid_down),
                 (up, 1, 1, grid_up), (down, 0, 1, grid_down),
@@ -254,7 +278,7 @@
             )
             self.copies = [
                 remote(
-                    part(chunk, quarter, late, way), self.buffers[kind].at[number % 2],
+                    part(0, quarter, late, way), self.buffers[kind].at[number % 2],
                     sent.at[number], received.at[number], to, b,
                 )
                 for number, (quarter, way, kind, to) in enumerate(routes)
@@ -271,38 +295,46 @@
         def second(self):
             for way, quarter in enumerate((up, down)):
                 self.copies[way].wait_recv()
-                ref = part(self.at[0], quarter, self.at[1], way)
+                ref = part(0, quarter, self.late, way)
                 ref[...] = ref[...] + self.buffers[0][way]
                 self.copies[4 + way].start()
 
         def spread(self):
-            chunk, late = self.at
             for copy in self.copies[2:]:
                 copy.wait_recv()
             for way in range(2):
-                x_sum[chunk, pl.ds(late * HALF + way * PIECE, PIECE)] = (
-                    part(chunk, x, late, way)[...]
+                x_sum[0, pl.ds(self.late * HALF + way * PIECE, PIECE)] = (
+                    part(0, x, self.late, way)[...]
                     + self.buffers[2][way]
                     + self.buffers[1][1 - way]
                 )
-            mine = pl.ds(pl.multiple_of(q * 8, 8), 8)
-            for owner_z in ((0, 1, 2, 3), (4, 7, 5, 6))[late]:
-                for owner_h in range(2):
-                    for owner_c in (1, 0):
-                        to = late * 16 + owner_h * 8 + owner_z % 4 * 2 + owner_c
-                        theirs = pl.ds(to * 8, 8)
-                        owner = x * SIDE + (owner_h * AZ + owner_z) * AC + owner_c
-
-                        @pl.when(q != to)
-                        def _(theirs=theirs, owner=owner):
-                            remote(
-                                x_sum.at[chunk, theirs], tiles.at[chunk, mine],
-                                z_send.at[chunk], z_recv.at[chunk], owner, b,
-                            ).start()
-
-            @pl.when(lax.div(z, 4) == late)
-            def _():
-                tiles[chunk, mine] = x_sum[chunk, mine]
+            send_tiles(0, self.late)
+
+    class Direct:
+        def __init__(self, late):
+            self.late = late
+            routes = ((across, across * SIDE + j), (up, grid_up), (down, grid_down))
+            self.copies = [
+                remote(
+                    whole(quarter, late), from_all.at[late, number],
+                    x_send.at[1, late, number], x_recv.at[1, late, number], to, b,
+                )
+                for number, (quarter, to) in enumerate(routes)
+            ]
+
+        def start(self):
+            for copy in self.copies:
+                copy.start()
+
+        def spread(self):
+            for copy in self.copies:
+                copy.wait_recv()
+            x_sum[1, pl.ds(self.late * HALF, HALF)] = (
+                whole(x, self.late)[...]
+                + from_all[self.late, 0]
+                + (from_all[self.late, 1] + from_all[self.late, 2])
+            )
+            send_tiles(1, self.late)
 
     def z_wait(buffer, chunk, sem):
         many = buffer.at[chunk, pl.ds(0, (SIDE - 1) * 8)]
@@ -322,9 +354,8 @@
             values.append(lanes(total, index) * factor)
         return values
 
-    (native, native_late), (distant, distant_late) = (
-        [Hop(chunk, late) for late in range(2)] for chunk in range(2)
-    )
+    native, native_late = Relay(0), Relay(1)
+    distant, distant_late = Direct(0), Direct(1)
 
     @pl.when(c == 0)
     def _():
@@ -355,32 +386,35 @@
         tell(3)
 
     distant_both()
-    distant.first()
 
     @pl.when(c == 0)
     def _():
+        hear(2)
+
+    @pl.when(c == 0)
+    def _():
         native.second()
+        distant.start()
         native_late.second()
-        distant_late.first()
-        distant.direct()
-        hear(2)
-        distant.second()
-        hear(3)
-        native.spread()
+
+    @pl.when(c == 1)
+    def _():
+        distant.start()
+
+    hear(3)
+    native.spread()
+
+    @pl.when(c == 1)
+    def _():
         native_late.spread()
 
-    @pl.when(c == 1)
-    def _():
-        hear(3)
-        native.spread()
-        distant_late.first()
-        distant.direct()
+    distant.spread()
+    distant_late.start()
+
+    @pl.when(c == 0)
+    def _():
         native_late.spread()
-        distant.second()
-
-    distant.spread()
-    distant_late.direct()
-    distant_late.second()
+
     distant_late.spread()
     values = z_last(0)
     values = values + z_last(1)
@@ -425,9 +459,10 @@
             pltpu.VMEM((2, 2, NG, NG), F32),
             pltpu.VMEM((8, NG, NG), F32),
             pltpu.VMEM((2, AX * QUARTER, NG), F32),
-            pltpu.VMEM((2, 2, 2, PIECE, NG), F32),
-            pltpu.VMEM((2, 2, 2, PIECE, NG), F32),
-            pltpu.VMEM((2, 2, 2, PIECE, NG), F32),
+            pltpu.VMEM((2, 2, PIECE, NG), F32),
+            pltpu.VMEM((2, 2, PIECE, NG), F32),
+            pltpu.VMEM((2, 2, PIECE, NG), F32),
+            pltpu.VMEM((2, 3, HALF, NG), F32),
             pltpu.VMEM((2, QUARTER, NG), F32),
             pltpu.VMEM((2, QUARTER, NG), F32),
             pltpu.SMEM((4,), jnp.int32),

time: 30.4 us -> 29.4 us (0.967)
  Pallas kernels: 29.7 us -> 28.7 us
    pallas_call x1, Pallas kernels: 29.7 us -> 28.7 us  [local(): pl.pallas_call(kernel, name='pair_sums', out_shape=pltpu.VMEM((32, NG), F...]
where the time goes in v8:
time: 29.4 us; the launch traced here: 29.3 us
  Pallas kernels  28.7 us (98%)
  local copies, waits for them, and re-layouts  0.61 us (2%)
    pallas_call x1, Pallas kernels, local(): pl.pallas_call(kernel, name='pair_sums', out_shape=pltpu.VMEM((32, NG), F...  28.7 us
    unnamed x1, local copies, waits for them, and re-layouts  0.61 us

profile of v8, /device:TPU:1, one launch (start us, length us, event | category | flops | bytes accessed | tf_op | source)
XLA Modules:
  0.0 29.3 jit_solution(16630464260907429017)
XLA Ops:
  0.0 28.7 %pair_sums.1 = f32[32,128]{1,0:T(8,128)S(1)} custom-call(s32[4]{0:T(128)} %order_ref.1, f32[2,4,128,128]{3,2,1,0:T(8,128)} %bitcast.5, f32[2,2,128,128]{3,2,1,0:T(8,128)} %bitcast.6, s32[4,4,8,128]{3,2,1,0:T(8,128)} %bitcast.7, bf16[768,256]{1,0:T(8,128)(2,1)} %constant.6.clone.along_x_ref, bf16[256,768]{1,0:T(8,128)(2,1)} %constant.7.clone.along_y_ref, ...), custom_call_target="tpu_custom_call" | custom-call | tf_op jit(solution)/shard_map/pair_sums/pallas_call | solution.py:442
  28.7 0.6 %copy.9 = f32[2,4,4,128]{3,2,1,0:T(4,128)} copy(f32[2,4,4,128]{3,2,1,0:T(4,128)S(1)} %bitcast.4) | data formatting | bytes 32768

commit v9 on v8

--- a/solution.py
+++ b/solution.py
@@ -18,6 +18,7 @@
 HALF = QUARTER // 2
 PIECE = HALF // 2
 PLACE = (0, 2, 1, 3)
+Y_ROWS = (6 * NG, 8 * NG, 10 * NG)
 MESH = pl.DeviceIdType.MESH
 F32 = jnp.float32
 BF16 = jnp.bfloat16
@@ -41,10 +42,10 @@
     high, low = halves(np.block([[cosine, -sine], [sine, cosine]]))
     along_x = np.concatenate([high, high, low], axis=0)
     high, low = halves(np.block([[cosine, sine], [-sine, cosine]]))
-    along_y = np.concatenate([high, low, high], axis=1)
+    along_y = np.concatenate([high, low, high], axis=0)
     trig = np.zeros((8, NG), np.float32)
     trig[0], trig[1] = cosine[1], sine[1]
-    return along_x, along_y, trig
+    return np.concatenate([along_x, along_y], axis=0), trig
 
 
 def lanes(value, index):
@@ -52,10 +53,11 @@
 
 
 def kernel(
-    order_ref, left_ref, right_ref, sphere_ref, along_x_ref, along_y_ref, trig_ref, out_ref,
-    lefts, rights, own_right, sphere, along_x, along_y, trig,
-    ky_t, val_t, kx_of, phase, acc, send, from_a, from_b, from_c, from_all, x_sum, tiles,
-    order, load_sem, pair_send, pair_recv, y_send, y_recv, x_send, x_recv, z_send, z_recv, known,
+    order_ref, left_ref, right_ref, sphere_ref, table_ref, trig_ref, out_ref,
+    lefts, rights, own_right, sphere, dft, trig,
+    ky_t, val_t, kx_of, phase, acc, send, from_a, from_bc, from_all, x_sum, tiles,
+    order, load_sem, pair_send, pair_recv, y_send, y_recv, native_send, native_recv, distant_send, distant_recv,
+    z_send, z_recv, known,
 ):
     g = lax.axis_index("grid")
     b = lax.axis_index("band")
@@ -71,17 +73,14 @@
         pltpu.make_async_copy(left_ref, lefts.at[c], load_sem.at[1]),
         pltpu.make_async_copy(trig_ref, trig, load_sem.at[2]),
         pltpu.make_async_copy(right_ref.at[:, c], rights.at[0, c], load_sem.at[3]),
-        pltpu.make_async_copy(along_x_ref, along_x, load_sem.at[4]),
-        pltpu.make_async_copy(along_y_ref, along_y, load_sem.at[5]),
-        pltpu.make_async_copy(order_ref, order, load_sem.at[6]),
+        pltpu.make_async_copy(table_ref, dft, load_sem.at[4]),
+        pltpu.make_async_copy(order_ref, order, load_sem.at[5]),
     ]
-    loads += [
-        pltpu.make_async_copy(
-            sphere_ref.at[:, at], sphere.at[:, PLACE[at]], load_sem.at[8 + at]
-        )
+    sphere_loads = [
+        pltpu.make_async_copy(sphere_ref.at[:, at], sphere.at[:, PLACE[at]], load_sem.at[6])
         for at in range(4)
     ]
-    for load in loads:
+    for load in loads[:1] + sphere_loads + loads[1:]:
         load.start()
 
     grid_up = up * SIDE + j
@@ -123,7 +122,7 @@
         )
 
     to_other = [
-        remote(own_right.at[:, m], rights.at[1, c], y_send.at[m], y_recv.at[c], g - c + m, 1 - b)
+        remote(own_right.at[:, m], rights.at[1, c], y_send, y_recv.at[c], g - c + m, 1 - b)
         for m in range(2)
     ]
     to_pair = [
@@ -139,8 +138,7 @@
         copy.start()
     tell(0)
 
-    for load in loads[7:]:
-        load.wait()
+    pltpu.make_async_copy(sphere, sphere, load_sem.at[6]).wait()
     loads[2].wait()
     flipped = sphere[...].reshape(NG, NG).T
     ky_t[...] = (flipped >> 7) & 127
@@ -177,7 +175,7 @@
             high, low = split(field)
             moved = jnp.dot(
                 jnp.concatenate([high, low, high], axis=1),
-                along_x[...],
+                dft[: 6 * NG, :],
                 preferred_element_type=F32,
             )
             columns.append(jnp.concatenate([moved[:, :NX], moved[:, NX:]], axis=0))
@@ -186,7 +184,9 @@
     def along_columns(rows):
         high, low = rows
         return jnp.dot(
-            along_y[...], jnp.concatenate([high, high, low], axis=0), preferred_element_type=F32
+            jnp.concatenate([dft[start : start + 2 * NG, :] for start in Y_ROWS], axis=1),
+            jnp.concatenate([high, high, low], axis=0),
+            preferred_element_type=F32,
         )
 
     def pick(plane, waves, half):
@@ -229,7 +229,7 @@
         waves = [along_columns(value) for value in rows]
         total(1, waves)
 
-    for load in loads[3:6]:
+    for load in loads[3:5]:
         load.wait()
     native_first(c)
     hear(0)
@@ -242,46 +242,43 @@
         start = pl.multiple_of(quarter * QUARTER + late * HALF + way * PIECE, PIECE)
         return send.at[chunk, pl.ds(start, PIECE)]
 
-    def whole(quarter, late):
-        start = pl.multiple_of(quarter * QUARTER + late * HALF, HALF)
-        return send.at[1, pl.ds(start, HALF)]
-
-    def send_tiles(chunk, late):
+    def send_tiles(chunk, places):
         mine = pl.ds(pl.multiple_of(q * 8, 8), 8)
-        for owner_z in ((0, 1, 2, 3), (4, 7, 5, 6))[late]:
-            for owner_h in range(2):
-                for owner_c in (1, 0):
-                    to = late * 16 + owner_h * 8 + owner_z % 4 * 2 + owner_c
-                    theirs = pl.ds(to * 8, 8)
-                    owner = x * SIDE + (owner_h * AZ + owner_z) * AC + owner_c
-
-                    @pl.when(q != to)
-                    def _(theirs=theirs, owner=owner):
-                        remote(
-                            x_sum.at[chunk, theirs], tiles.at[chunk, mine],
-                            z_send.at[chunk], z_recv.at[chunk], owner, b,
-                        ).start()
-
-        @pl.when(lax.div(z, 4) == late)
+        for to in places:
+            owner_z = to // 16 * 4 + to % 8 // AC
+            theirs = pl.ds(to * 8, 8)
+            owner = x * SIDE + (to % 16 // 8 * AZ + owner_z) * AC + to % AC
+
+            @pl.when(q != to)
+            def _(theirs=theirs, owner=owner):
+                remote(
+                    x_sum.at[chunk, theirs], tiles.at[chunk, mine],
+                    z_send.at[chunk], z_recv.at[chunk], owner, b,
+                ).start()
+
+        @pl.when(functools.reduce(jnp.logical_or, [q == to for to in places]))
         def _():
             tiles[chunk, mine] = x_sum[chunk, mine]
 
     class Relay:
         def __init__(self, late):
             self.late = late
-            sent, received = x_send.at[0, late], x_recv.at[0, late]
-            self.buffers = [ref.at[late] for ref in (from_a, from_b, from_c)]
+            self.added = from_a.at[late]
+            self.last = from_bc.at[late]
             routes = (
-                (across, 0, 0, grid_up), (across, 1, 0, grid_down),
-                (up, 1, 1, grid_up), (down, 0, 1, grid_down),
-                (up, 0, 2, grid_up), (down, 1, 2, grid_down),
+                (across, 0, self.added.at[0], 0, grid_up),
+                (across, 1, self.added.at[1], 1, grid_down),
+                (up, 1, self.last.at[0], 2, grid_up),
+                (down, 0, self.last.at[1], 2, grid_down),
+                (up, 0, self.last.at[2], 2, grid_up),
+                (down, 1, self.last.at[3], 2, grid_down),
             )
             self.copies = [
                 remote(
-                    part(0, quarter, late, way), self.buffers[kind].at[number % 2],
-                    sent.at[number], received.at[number], to, b,
+                    part(0, quarter, late, way), target, native_send,
+                    native_recv.at[late, number], to, b,
                 )
-                for number, (quarter, way, kind, to) in enumerate(routes)
+                for quarter, way, target, number, to in routes
             ]
 
         def first(self):
@@ -296,45 +293,55 @@
             for way, quarter in enumerate((up, down)):
                 self.copies[way].wait_recv()
                 ref = part(0, quarter, self.late, way)
-                ref[...] = ref[...] + self.buffers[0][way]
+                ref[...] = ref[...] + self.added[way]
                 self.copies[4 + way].start()
 
         def spread(self):
-            for copy in self.copies[2:]:
-                copy.wait_recv()
+            pltpu.make_async_copy(self.last, self.last, native_recv.at[self.late, 2]).wait()
             for way in range(2):
                 x_sum[0, pl.ds(self.late * HALF + way * PIECE, PIECE)] = (
-                    part(0, x, self.late, way)[...]
-                    + self.buffers[2][way]
-                    + self.buffers[1][1 - way]
+                    part(0, x, self.late, way)[...] + self.last[2 + way] + self.last[1 - way]
                 )
-            send_tiles(0, self.late)
+            send_tiles(
+                0,
+                [
+                    self.late * 16 + way * 8 + AC * at + core
+                    for at in range(4)
+                    for way in range(2)
+                    for core in (1, 0)
+                ],
+            )
 
     class Direct:
-        def __init__(self, late):
-            self.late = late
-            routes = ((across, across * SIDE + j), (up, grid_up), (down, grid_down))
-            self.copies = [
-                remote(
-                    whole(quarter, late), from_all.at[late, number],
-                    x_send.at[1, late, number], x_recv.at[1, late, number], to, b,
-                )
-                for number, (quarter, to) in enumerate(routes)
-            ]
+        def __init__(self, number, first, count):
+            self.places = range(first, first + count)
+            self.rows = pl.ds(first * 8, count * 8)
+            self.received = distant_recv.at[number]
+
+        def of_quarter(self, quarter):
+            start = pl.multiple_of(quarter * QUARTER + self.rows.start, 8)
+            return send.at[1, pl.ds(start, self.rows.size)]
 
         def start(self):
-            for copy in self.copies:
-                copy.start()
+            for owner_x in (0, 1, 3, 2):
+
+                @pl.when(x != owner_x)
+                def _(owner_x=owner_x):
+                    number = lax.rem(x - owner_x + AX, AX) - 1
+                    remote(
+                        self.of_quarter(owner_x), from_all.at[number, self.rows],
+                        distant_send, self.received, owner_x * SIDE + j, b,
+                    ).start()
 
         def spread(self):
-            for copy in self.copies:
-                copy.wait_recv()
-            x_sum[1, pl.ds(self.late * HALF, HALF)] = (
-                whole(x, self.late)[...]
-                + from_all[self.late, 0]
-                + (from_all[self.late, 1] + from_all[self.late, 2])
+            arrived = from_all.at[:, self.rows]
+            pltpu.make_async_copy(arrived, arrived, self.received).wait()
+            x_sum[1, self.rows] = (
+                self.of_quarter(x)[...]
+                + from_all[1, self.rows]
+                + (from_all[0, self.rows] + from_all[2, self.rows])
             )
-            send_tiles(1, self.late)
+            send_tiles(1, self.places)
 
     def z_wait(buffer, chunk, sem):
         many = buffer.at[chunk, pl.ds(0, (SIDE - 1) * 8)]
@@ -355,7 +362,10 @@
         return values
 
     native, native_late = Relay(0), Relay(1)
-    distant, distant_late = Direct(0), Direct(1)
+    distant = [
+        Direct(number, first, count)
+        for number, (first, count) in enumerate(((0, 2), (2, 6), (8, 8), (16, 16)))
+    ]
 
     @pl.when(c == 0)
     def _():
@@ -375,7 +385,7 @@
 
     def arrival(core):
         return remote(
-            own_right.at[:, 0], rights.at[1, core], y_send.at[0], y_recv.at[core], g, 1 - b
+            own_right.at[:, 0], rights.at[1, core], y_send, y_recv.at[core], g, 1 - b
         )
 
     arrival(0).wait_recv()
@@ -391,34 +401,47 @@
     def _():
         hear(2)
 
+    distant[0].start()
+
     @pl.when(c == 0)
     def _():
         native.second()
-        distant.start()
+        distant[1].start()
+        distant[2].start()
         native_late.second()
 
     @pl.when(c == 1)
     def _():
-        distant.start()
+        distant[1].start()
 
     hear(3)
     native.spread()
 
     @pl.when(c == 1)
     def _():
+        distant[2].start()
         native_late.spread()
 
-    distant.spread()
-    distant_late.start()
+    @pl.when(jnp.logical_or(c == 0, z < 4))
+    def _():
+        distant[3].start()
+
+    distant[0].spread()
+    distant[1].spread()
+    distant[2].spread()
+
+    @pl.when(jnp.logical_and(c == 1, z >= 4))
+    def _():
+        distant[3].start()
 
     @pl.when(c == 0)
     def _():
         native_late.spread()
 
-    distant_late.spread()
+    distant[3].spread()
     values = z_last(0)
     values = values + z_last(1)
-    loads[6].wait()
+    loads[5].wait()
     for column in range(4):
         position = jnp.full((8, NG), lax.rem(order[column] + 4 - 2 * b, 4), jnp.int32)
         value = values[3]
@@ -426,32 +449,32 @@
             value = jnp.where(position == at, values[at], value)
         out_ref[pl.ds(column, 8, stride=4), :] = value
 
-    for copy in to_pair + to_other:
+    for copy in to_pair:
         copy.wait_send()
-    for hop in (native, native_late, distant, distant_late):
-        for copy in hop.copies:
-            copy.wait_send()
+    pltpu.make_async_copy(own_right, own_right, y_send).wait()
+    for chunk, sem in enumerate((native_send, distant_send)):
+        sent = send.at[chunk, pl.ds(0, 3 * QUARTER)]
+        pltpu.make_async_copy(sent, sent, sem).wait()
     for chunk in range(2):
         z_wait(x_sum, chunk, z_send)
 
 
 def local(left_bands, right_bands, sphere_index, right_order):
-    along_x, along_y, trig = dft_tables()
+    table, trig = dft_tables()
     hbm = pl.BlockSpec(memory_space=pltpu.HBM)
     dma = pltpu.SemaphoreType.DMA
     result = pl.pallas_call(
         kernel,
         name="pair_sums",
         out_shape=pltpu.VMEM((32, NG), F32),
-        in_specs=[hbm] * 7,
+        in_specs=[hbm] * 6,
         out_specs=pl.BlockSpec(memory_space=pltpu.VMEM),
         scratch_shapes=[
             pltpu.VMEM((2, 2, 4, NG, NX), F32),
             pltpu.VMEM((2, 2, 2, NG, NX), F32),
             pltpu.VMEM((2, 2, NG, NX), F32),
             pltpu.VMEM((4, 4, 8, NG), jnp.int32),
-            pltpu.VMEM((6 * NG, 2 * NG), BF16),
-            pltpu.VMEM((2 * NG, 6 * NG), BF16),
+            pltpu.VMEM((12 * NG, 2 * NG), BF16),
             pltpu.VMEM((8, NG), F32),
             pltpu.VMEM((NG, NG), jnp.int32),
             pltpu.VMEM((NG, NG), jnp.int32),
@@ -460,14 +483,13 @@
             pltpu.VMEM((8, NG, NG), F32),
             pltpu.VMEM((2, AX * QUARTER, NG), F32),
             pltpu.VMEM((2, 2, PIECE, NG), F32),
-            pltpu.VMEM((2, 2, PIECE, NG), F32),
-            pltpu.VMEM((2, 2, PIECE, NG), F32),
-            pltpu.VMEM((2, 3, HALF, NG), F32),
+            pltpu.VMEM((2, 4, PIECE, NG), F32),
+            pltpu.VMEM((3, QUARTER, NG), F32),
             pltpu.VMEM((2, QUARTER, NG), F32),
             pltpu.VMEM((2, QUARTER, NG), F32),
             pltpu.SMEM((4,), jnp.int32),
-            dma((12,)), dma((2,)), dma((2,)), dma((2,)), dma((2,)),
-            dma((2, 2, 6)), dma((2, 2, 6)), dma((2,)), dma((2,)), pltpu.SemaphoreType.REGULAR((4,)),
+            dma((7,)), dma((2,)), dma((2,)), dma, dma((2,)), dma, dma((2, 3)), dma, dma((4,)),
+            dma((2,)), dma((2,)), pltpu.SemaphoreType.REGULAR((4,)),
         ],
         compiler_params=pltpu.CompilerParams(collective_id=0, has_side_effects=True),
     )(
@@ -475,8 +497,7 @@
         left_bands.reshape(2, 4, NG, NX),
         right_bands.reshape(2, 2, NG, NX),
         sphere_index.reshape(4, 4, 8, NG),
-        jnp.asarray(along_x),
-        jnp.asarray(along_y),
+        jnp.asarray(table),
         jnp.asarray(trig),
     )
     return result.reshape(2, 4, 4, NG)

time: 29.4 us -> 28.1 us (0.956)
  Pallas kernels: 28.7 us -> 27.4 us
    pallas_call x1, Pallas kernels: 28.7 us -> 27.4 us  [local(): pl.pallas_call(kernel, name='pair_sums', out_shape=pltpu.VMEM((32, NG), F...]
where the time goes in v9:
time: 28.1 us; the launch traced here: 28 us
  Pallas kernels  27.4 us (98%)
  local copies, waits for them, and re-layouts  0.61 us (2%)
    pallas_call x1, Pallas kernels, local(): pl.pallas_call(kernel, name='pair_sums', out_shape=pltpu.VMEM((32, NG), F...  27.4 us
    unnamed x1, local copies, waits for them, and re-layouts  0.61 us

profile of v9, /device:TPU:1, one launch (start us, length us, event | category | flops | bytes accessed | tf_op | source)
XLA Modules:
  0.0 28.0 jit_solution(9034877793404851627)
XLA Ops:
  0.0 27.4 %pair_sums.1 = f32[32,128]{1,0:T(8,128)S(1)} custom-call(s32[4]{0:T(128)} %order_ref.1, f32[2,4,128,128]{3,2,1,0:T(8,128)} %bitcast.5, f32[2,2,128,128]{3,2,1,0:T(8,128)} %bitcast.6, s32[4,4,8,128]{3,2,1,0:T(8,128)} %bitcast.7, bf16[1536,256]{1,0:T(8,128)(2,1)} %constant.4.clone.table_ref, f32[8,128]{1,0:T(8,128)} %constant.5.clone.trig_ref), custom_call_target="tpu_custom_call" | custom-call | tf_op jit(solution)/shard_map/pair_sums/pallas_call | solution.py:466
  27.4 0.6 %copy.8 = f32[2,4,4,128]{3,2,1,0:T(4,128)} copy(f32[2,4,4,128]{3,2,1,0:T(4,128)S(1)} %bitcast.4) | data formatting | bytes 32768

commit v10 on v9

--- a/solution.py
+++ b/solution.py
@@ -161,24 +161,27 @@
     def along_rows(chunk, plane, half):
         right_real = rights[chunk, plane, 0]
         right_imag = rights[chunk, plane, 1]
-        columns = []
+        fields = []
         for n in (2 * half, 2 * half + 1):
             left_real = lefts[plane, 0, n]
             left_imag = lefts[plane, 1, n]
-            field = jnp.concatenate(
-                [
-                    left_real * right_real + left_imag * right_imag,
-                    left_real * right_imag - left_imag * right_real,
-                ],
-                axis=1,
+            fields.append(
+                jnp.concatenate(
+                    [
+                        left_real * right_real + left_imag * right_imag,
+                        left_real * right_imag - left_imag * right_real,
+                    ],
+                    axis=1,
+                )
             )
-            high, low = split(field)
-            moved = jnp.dot(
-                jnp.concatenate([high, low, high], axis=1),
-                dft[: 6 * NG, :],
-                preferred_element_type=F32,
-            )
-            columns.append(jnp.concatenate([moved[:, :NX], moved[:, NX:]], axis=0))
+        high, low = split(jnp.concatenate(fields, axis=0))
+        moved = jnp.dot(
+            jnp.concatenate([high, low, high], axis=1), dft[: 6 * NG, :], preferred_element_type=F32
+        )
+        columns = [
+            jnp.concatenate([moved[start : start + NG, :NX], moved[start : start + NG, NX:]], axis=0)
+            for start in (0, NG)
+        ]
         return split(jnp.concatenate(columns, axis=1))
 
     def along_columns(rows):
@@ -222,12 +225,10 @@
             for channel in first:
                 ship(1, channel, first[channel] + second[channel])
 
-        rows = [along_rows(1, plane, 0) for plane in range(2)]
+        rows = [along_rows(1, plane, half) for half in range(2) for plane in range(2)]
         waves = [along_columns(value) for value in rows]
-        rows = [along_rows(1, plane, 1) for plane in range(2)]
-        total(0, waves)
-        waves = [along_columns(value) for value in rows]
-        total(1, waves)
+        total(0, waves[:2])
+        total(1, waves[2:])
 
     for load in loads[3:5]:
         load.wait()
@@ -420,13 +421,12 @@
     @pl.when(c == 1)
     def _():
         distant[2].start()
-        native_late.spread()
+
+    distant[0].spread()
 
     @pl.when(jnp.logical_or(c == 0, z < 4))
     def _():
         distant[3].start()
-
-    distant[0].spread()
     distant[1].spread()
     distant[2].spread()
 
@@ -434,10 +434,7 @@
     def _():
         distant[3].start()
 
-    @pl.when(c == 0)
-    def _():
-        native_late.spread()
-
+    native_late.spread()
     distant[3].spread()
     values = z_last(0)
     values = values + z_last(1)

time: 28.1 us -> 28.3 us (level)
  no operation moved by 1% of the time
where the time goes in v10:
time: 28.3 us; the launch traced here: 28.2 us
  Pallas kernels  27.6 us (98%)
  local copies, waits for them, and re-layouts  0.61 us (2%)
    pallas_call x1, Pallas kernels, local(): pl.pallas_call(kernel, name='pair_sums', out_shape=pltpu.VMEM((32, NG), F...  27.6 us
    unnamed x1, local copies, waits for them, and re-layouts  0.61 us

profile of v10, /device:TPU:1, one launch (start us, length us, event | category | flops | bytes accessed | tf_op | source)
XLA Modules:
  0.0 28.2 jit_solution(3970159211877382828)
XLA Ops:
  0.0 27.6 %pair_sums.1 = f32[32,128]{1,0:T(8,128)S(1)} custom-call(s32[4]{0:T(128)} %order_ref.1, f32[2,4,128,128]{3,2,1,0:T(8,128)} %bitcast.5, f32[2,2,128,128]{3,2,1,0:T(8,128)} %bitcast.6, s32[4,4,8,128]{3,2,1,0:T(8,128)} %bitcast.7, bf16[1536,256]{1,0:T(8,128)(2,1)} %constant.4.clone.table_ref, f32[8,128]{1,0:T(8,128)} %constant.5.clone.trig_ref), custom_call_target="tpu_custom_call" | custom-call | tf_op jit(solution)/shard_map/pair_sums/pallas_call | solution.py:463
  27.6 0.6 %copy.8 = f32[2,4,4,128]{3,2,1,0:T(4,128)} copy(f32[2,4,4,128]{3,2,1,0:T(4,128)S(1)} %bitcast.4) | data formatting | bytes 32768

commit v11 on v10

--- a/solution.py
+++ b/solution.py
@@ -56,8 +56,7 @@
     order_ref, left_ref, right_ref, sphere_ref, table_ref, trig_ref, out_ref,
     lefts, rights, own_right, sphere, dft, trig,
     ky_t, val_t, kx_of, phase, acc, send, from_a, from_bc, from_all, x_sum, tiles,
-    order, load_sem, pair_send, pair_recv, y_send, y_recv, native_send, native_recv, distant_send, distant_recv,
-    z_send, z_recv, known,
+    order, load_sem, early_send, pair_recv, y_recv, send_sem, native_recv, distant_recv, z_recv, known,
 ):
     g = lax.axis_index("grid")
     b = lax.axis_index("band")
@@ -122,12 +121,12 @@
         )
 
     to_other = [
-        remote(own_right.at[:, m], rights.at[1, c], y_send, y_recv.at[c], g - c + m, 1 - b)
+        remote(own_right.at[:, m], rights.at[1, c], early_send, y_recv, g - c + m, 1 - b)
         for m in range(2)
     ]
     to_pair = [
-        remote(lefts.at[c], lefts.at[c], pair_send.at[0], pair_recv.at[0], pair, b),
-        remote(own_right.at[:, 1 - c], rights.at[0, c], pair_send.at[1], pair_recv.at[1], pair, b),
+        remote(lefts.at[c], lefts.at[c], early_send, pair_recv, pair, b),
+        remote(own_right.at[:, 1 - c], rights.at[0, c], early_send, pair_recv, pair, b),
     ]
     loads[0].wait()
     pl.semaphore_wait(barrier, jnp.where(c == 1, len(close) + len(near), len(close)))
@@ -235,8 +234,8 @@
     native_first(c)
     hear(0)
     tell(1)
-    for copy in to_pair:
-        copy.wait_recv()
+    both = send.at[:, pl.ds(0, 640)]
+    pltpu.make_async_copy(both, both, pair_recv).wait()
     native_second(1 - c)
 
     def part(chunk, quarter, late, way):
@@ -254,7 +253,7 @@
             def _(theirs=theirs, owner=owner):
                 remote(
                     x_sum.at[chunk, theirs], tiles.at[chunk, mine],
-                    z_send.at[chunk], z_recv.at[chunk], owner, b,
+                    send_sem, z_recv.at[chunk], owner, b,
                 ).start()
 
         @pl.when(functools.reduce(jnp.logical_or, [q == to for to in places]))
@@ -268,15 +267,15 @@
             self.last = from_bc.at[late]
             routes = (
                 (across, 0, self.added.at[0], 0, grid_up),
-                (across, 1, self.added.at[1], 1, grid_down),
-                (up, 1, self.last.at[0], 2, grid_up),
-                (down, 0, self.last.at[1], 2, grid_down),
-                (up, 0, self.last.at[2], 2, grid_up),
-                (down, 1, self.last.at[3], 2, grid_down),
+                (across, 1, self.added.at[1], 0, grid_down),
+                (up, 1, self.last.at[0], 1, grid_up),
+                (down, 0, self.last.at[1], 1, grid_down),
+                (up, 0, self.last.at[2], 1, grid_up),
+                (down, 1, self.last.at[3], 1, grid_down),
             )
             self.copies = [
                 remote(
-                    part(0, quarter, late, way), target, native_send,
+                    part(0, quarter, late, way), target, send_sem,
                     native_recv.at[late, number], to, b,
                 )
                 for quarter, way, target, number, to in routes
@@ -291,14 +290,14 @@
                 copy.start()
 
         def second(self):
+            pltpu.make_async_copy(self.added, self.added, native_recv.at[self.late, 0]).wait()
             for way, quarter in enumerate((up, down)):
-                self.copies[way].wait_recv()
                 ref = part(0, quarter, self.late, way)
                 ref[...] = ref[...] + self.added[way]
                 self.copies[4 + way].start()
 
         def spread(self):
-            pltpu.make_async_copy(self.last, self.last, native_recv.at[self.late, 2]).wait()
+            pltpu.make_async_copy(self.last, self.last, native_recv.at[self.late, 1]).wait()
             for way in range(2):
                 x_sum[0, pl.ds(self.late * HALF + way * PIECE, PIECE)] = (
                     part(0, x, self.late, way)[...] + self.last[2 + way] + self.last[1 - way]
@@ -331,7 +330,7 @@
                     number = lax.rem(x - owner_x + AX, AX) - 1
                     remote(
                         self.of_quarter(owner_x), from_all.at[number, self.rows],
-                        distant_send, self.received, owner_x * SIDE + j, b,
+                        send_sem, self.received, owner_x * SIDE + j, b,
                     ).start()
 
         def spread(self):
@@ -344,16 +343,16 @@
             )
             send_tiles(1, self.places)
 
-    def z_wait(buffer, chunk, sem):
-        many = buffer.at[chunk, pl.ds(0, (SIDE - 1) * 8)]
-        pltpu.make_async_copy(many, many, sem.at[chunk]).wait()
+    def z_wait(chunk):
+        many = tiles.at[chunk, pl.ds(0, (SIDE - 1) * 8)]
+        pltpu.make_async_copy(many, many, z_recv.at[chunk]).wait()
 
     own = sphere[x, lax.div(z, 4) * 2 + h, pl.ds(lax.rem(z, 4) * AC + c, 1), :]
     index = jnp.broadcast_to((own >> 7) & 127, (8, NG))
     factor = 1.0 / (NG * NG * NX) ** 0.5
 
     def z_last(chunk):
-        z_wait(tiles, chunk, z_recv)
+        z_wait(chunk)
         values = []
         for core in range(2):
             total = tiles[chunk, pl.ds(core * 8, 8)]
@@ -384,13 +383,7 @@
         native.second()
         native_late.second()
 
-    def arrival(core):
-        return remote(
-            own_right.at[:, 0], rights.at[1, core], y_send, y_recv.at[core], g, 1 - b
-        )
-
-    arrival(0).wait_recv()
-    arrival(1).wait_recv()
+    pltpu.make_async_copy(rights.at[1], rights.at[1], y_recv).wait()
     @pl.when(c == 1)
     def _():
         hear(2)
@@ -446,14 +439,9 @@
             value = jnp.where(position == at, values[at], value)
         out_ref[pl.ds(column, 8, stride=4), :] = value
 
-    for copy in to_pair:
-        copy.wait_send()
-    pltpu.make_async_copy(own_right, own_right, y_send).wait()
-    for chunk, sem in enumerate((native_send, distant_send)):
-        sent = send.at[chunk, pl.ds(0, 3 * QUARTER)]
+    for sem, rows in ((early_send, 896), (send_sem, 1016)):
+        sent = send.at[:, pl.ds(0, rows)]
         pltpu.make_async_copy(sent, sent, sem).wait()
-    for chunk in range(2):
-        z_wait(x_sum, chunk, z_send)
 
 
 def local(left_bands, right_bands, sphere_index, right_order):
@@ -485,8 +473,8 @@
             pltpu.VMEM((2, QUARTER, NG), F32),
             pltpu.VMEM((2, QUARTER, NG), F32),
             pltpu.SMEM((4,), jnp.int32),
-            dma((7,)), dma((2,)), dma((2,)), dma, dma((2,)), dma, dma((2, 3)), dma, dma((4,)),
-            dma((2,)), dma((2,)), pltpu.SemaphoreType.REGULAR((4,)),
+            dma((7,)), dma, dma, dma, dma, dma((2, 2)), dma((4,)), dma((2,)),
+            pltpu.SemaphoreType.REGULAR((4,)),
         ],
         compiler_params=pltpu.CompilerParams(collective_id=0, has_side_effects=True),
     )(

time: 28.3 us -> 27.9 us (0.986)
  Pallas kernels: 27.6 us -> 27.2 us
    pallas_call x1, Pallas kernels: 27.6 us -> 27.2 us  [local(): pl.pallas_call(kernel, name='pair_sums', out_shape=pltpu.VMEM((32, NG), F...]
where the time goes in v11:
time: 27.9 us; the launch traced here: 27.8 us
  Pallas kernels  27.2 us (97%)
  local copies, waits for them, and re-layouts  0.61 us (2%)
    pallas_call x1, Pallas kernels, local(): pl.pallas_call(kernel, name='pair_sums', out_shape=pltpu.VMEM((32, NG), F...  27.2 us
    unnamed x1, local copies, waits for them, and re-layouts  0.61 us

profile of v11, /device:TPU:1, one launch (start us, length us, event | category | flops | bytes accessed | tf_op | source)
XLA Modules:
  0.0 27.8 jit_solution(11768937777161321860)
XLA Ops:
  0.0 27.2 %pair_sums.1 = f32[32,128]{1,0:T(8,128)S(1)} custom-call(s32[4]{0:T(128)} %order_ref.1, f32[2,4,128,128]{3,2,1,0:T(8,128)} %bitcast.5, f32[2,2,128,128]{3,2,1,0:T(8,128)} %bitcast.6, s32[4,4,8,128]{3,2,1,0:T(8,128)} %bitcast.7, bf16[1536,256]{1,0:T(8,128)(2,1)} %constant.4.clone.table_ref, f32[8,128]{1,0:T(8,128)} %constant.5.clone.trig_ref), custom_call_target="tpu_custom_call" | custom-call | tf_op jit(solution)/shard_map/pair_sums/pallas_call | solution.py:451
  27.2 0.6 %copy.8 = f32[2,4,4,128]{3,2,1,0:T(4,128)} copy(f32[2,4,4,128]{3,2,1,0:T(4,128)S(1)} %bitcast.4) | data formatting | bytes 32768

commit v12 on v11

--- a/solution.py
+++ b/solution.py
@@ -70,13 +70,13 @@
     loads = [
         pltpu.make_async_copy(right_ref, own_right, load_sem.at[0]),
         pltpu.make_async_copy(left_ref, lefts.at[c], load_sem.at[1]),
-        pltpu.make_async_copy(trig_ref, trig, load_sem.at[2]),
-        pltpu.make_async_copy(right_ref.at[:, c], rights.at[0, c], load_sem.at[3]),
-        pltpu.make_async_copy(table_ref, dft, load_sem.at[4]),
-        pltpu.make_async_copy(order_ref, order, load_sem.at[5]),
+        pltpu.make_async_copy(trig_ref, trig, load_sem.at[4]),
+        pltpu.make_async_copy(right_ref.at[:, c], rights.at[0, c], load_sem.at[2]),
+        pltpu.make_async_copy(table_ref, dft, load_sem.at[2]),
+        pltpu.make_async_copy(order_ref, order, load_sem.at[3]),
     ]
     sphere_loads = [
-        pltpu.make_async_copy(sphere_ref.at[:, at], sphere.at[:, PLACE[at]], load_sem.at[6])
+        pltpu.make_async_copy(sphere_ref.at[:, at], sphere.at[:, PLACE[at]], load_sem.at[4])
         for at in range(4)
     ]
     for load in loads[:1] + sphere_loads + loads[1:]:
@@ -137,8 +137,8 @@
         copy.start()
     tell(0)
 
-    pltpu.make_async_copy(sphere, sphere, load_sem.at[6]).wait()
-    loads[2].wait()
+    both = send.at[0, pl.ds(0, 136)]
+    pltpu.make_async_copy(both, both, load_sem.at[4]).wait()
     flipped = sphere[...].reshape(NG, NG).T
     ky_t[...] = (flipped >> 7) & 127
     val_t[...] = ((flipped >> 14) << 7) | (flipped & 127)
@@ -229,8 +229,8 @@
         total(0, waves[:2])
         total(1, waves[2:])
 
-    for load in loads[3:5]:
-        load.wait()
+    both = send.at[:, pl.ds(0, 896)]
+    pltpu.make_async_copy(both, both, load_sem.at[2]).wait()
     native_first(c)
     hear(0)
     tell(1)
@@ -473,7 +473,7 @@
             pltpu.VMEM((2, QUARTER, NG), F32),
             pltpu.VMEM((2, QUARTER, NG), F32),
             pltpu.SMEM((4,), jnp.int32),
-            dma((7,)), dma, dma, dma, dma, dma((2, 2)), dma((4,)), dma((2,)),
+            dma((5,)), dma, dma, dma, dma, dma((2, 2)), dma((4,)), dma((2,)),
             pltpu.SemaphoreType.REGULAR((4,)),
         ],
         compiler_params=pltpu.CompilerParams(collective_id=0, has_side_effects=True),

time: 27.9 us -> 27.9 us (level)
  no operation moved by 1% of the time
where the time goes in v12:
time: 27.9 us; the launch traced here: 27.8 us
  Pallas kernels  27.2 us (97%)
  local copies, waits for them, and re-layouts  0.61 us (2%)
    pallas_call x1, Pallas kernels, local(): pl.pallas_call(kernel, name='pair_sums', out_shape=pltpu.VMEM((32, NG), F...  27.2 us
    unnamed x1, local copies, waits for them, and re-layouts  0.61 us

profile of v12, /device:TPU:1, one launch (start us, length us, event | category | flops | bytes accessed | tf_op | source)
XLA Modules:
  0.0 27.8 jit_solution(10844113485200043612)
XLA Ops:
  0.0 27.2 %pair_sums.1 = f32[32,128]{1,0:T(8,128)S(1)} custom-call(s32[4]{0:T(128)} %order_ref.1, f32[2,4,128,128]{3,2,1,0:T(8,128)} %bitcast.5, f32[2,2,128,128]{3,2,1,0:T(8,128)} %bitcast.6, s32[4,4,8,128]{3,2,1,0:T(8,128)} %bitcast.7, bf16[1536,256]{1,0:T(8,128)(2,1)} %constant.4.clone.table_ref, f32[8,128]{1,0:T(8,128)} %constant.5.clone.trig_ref), custom_call_target="tpu_custom_call" | custom-call | tf_op jit(solution)/shard_map/pair_sums/pallas_call | solution.py:451
  27.2 0.6 %copy.8 = f32[2,4,4,128]{3,2,1,0:T(4,128)} copy(f32[2,4,4,128]{3,2,1,0:T(4,128)S(1)} %bitcast.4) | data formatting | bytes 32768

commit v13 on v12

--- a/solution.py
+++ b/solution.py
@@ -404,15 +404,13 @@
         distant[2].start()
         native_late.second()
 
-    @pl.when(c == 1)
-    def _():
-        distant[1].start()
 
     hear(3)
     native.spread()
 
     @pl.when(c == 1)
     def _():
+        distant[1].start()
         distant[2].start()
 
     distant[0].spread()

time: 27.9 us -> 28.5 us (1.022)
  Pallas kernels: 27.2 us -> 27.8 us
    pallas_call x1, Pallas kernels: 27.2 us -> 27.8 us  [local(): pl.pallas_call(kernel, name='pair_sums', out_shape=pltpu.VMEM((32, NG), F...]
where the time goes in v13:
time: 28.5 us
  Pallas kernels  27.8 us (98%)
  local copies, waits for them, and re-layouts  0.61 us (2%)
    pallas_call x1, Pallas kernels, local(): pl.pallas_call(kernel, name='pair_sums', out_shape=pltpu.VMEM((32, NG), F...  27.8 us
    unnamed x1, local copies, waits for them, and re-layouts  0.61 us

profile of v13, /device:TPU:1, one launch (start us, length us, event | category | flops | bytes accessed | tf_op | source)
XLA Modules:
  0.0 28.5 jit_solution(14401119803436058379)
XLA Ops:
  0.0 27.8 %pair_sums.1 = f32[32,128]{1,0:T(8,128)S(1)} custom-call(s32[4]{0:T(128)} %order_ref.1, f32[2,4,128,128]{3,2,1,0:T(8,128)} %bitcast.5, f32[2,2,128,128]{3,2,1,0:T(8,128)} %bitcast.6, s32[4,4,8,128]{3,2,1,0:T(8,128)} %bitcast.7, bf16[1536,256]{1,0:T(8,128)(2,1)} %constant.4.clone.table_ref, f32[8,128]{1,0:T(8,128)} %constant.5.clone.trig_ref), custom_call_target="tpu_custom_call" | custom-call | tf_op jit(solution)/shard_map/pair_sums/pallas_call | solution.py:449
  27.8 0.6 %copy.8 = f32[2,4,4,128]{3,2,1,0:T(4,128)} copy(f32[2,4,4,128]{3,2,1,0:T(4,128)S(1)} %bitcast.4) | data formatting | bytes 32768
